TPU v7x, 16 devices: a whole 2x2x2 slice. The times are simulated.
16 devices in a mesh: data: 4 (over z, y), stage: 4 (over x, core).
Axes of the slice: x: 2, y: 2, z: 2, core: 2. Of those that a mesh axis runs over, the one named last changes fastest.
Arguments:
- x: bfloat16 [64, 256, 768], P('data'), parts along dimension 0
- g: bfloat16 [64, 256, 768], P('data'), parts along dimension 0
- w1: bfloat16 [2, 4, 768, 3072], P(None, 'stage')
- w2: bfloat16 [2, 4, 3072, 768], P(None, 'stage')
Outputs:
- output 1: bfloat16 [64, 256, 768], P('data'), parts along dimension 0
- output 2: bfloat16 [64, 256, 768], P('data'), parts along dimension 0
- output 3: float32 [8, 4, 768, 3072], P('data', 'stage'), parts along dimension 0
- output 4: float32 [8, 4, 3072, 768], P('data', 'stage'), parts along dimension 0
There are 4 independent parts. A program takes and returns all parts, laid end to end along the dimension named above; an argument that names none is the same for every part.
All inputs are finite; a program needn't handle non-finite values.
Results may differ from a plain program's by a relative error of at most 0.02.
Values are sent between devices in bfloat16 or wider.
A program may use at most 1 GiB of HBM per device.

v0:
```python
import jax
import jax.numpy as jnp
from jax import lax
from jax.sharding import PartitionSpec as P


def _gelu(z):
    return 0.5 * z * (1.0 + lax.erf(z * 0.7071067811865476))


def _gelu_grad(z):
    return 0.5 * (1.0 + lax.erf(z * 0.7071067811865476)) + z * jnp.exp(-0.5 * z * z) * 0.3989422804014327


def _gelu_pair(z):
    e = lax.erf(z * 0.7071067811865476)
    return 0.5 * z * (1.0 + e), 0.5 * (1.0 + e) + z * jnp.exp(-0.5 * z * z) * 0.3989422804014327


def _fwd(h, w1, w2):
    z = jnp.dot(h, w1, preferred_element_type=jnp.float32)
    u = _gelu(z).astype(jnp.bfloat16)
    r = jnp.dot(u, w2, preferred_element_type=jnp.float32)
    return (h.astype(jnp.float32) + r).astype(jnp.bfloat16)


def _bwd(h, w1, w2, dy):
    nt = (((1,), (1,)), ((), ()))
    z = jnp.dot(h, w1, preferred_element_type=jnp.float32)
    a, b = _gelu_pair(z)
    u = a.astype(jnp.bfloat16)
    du = lax.dot_general(dy, w2, nt, preferred_element_type=jnp.float32)
    dz = (du * b).astype(jnp.bfloat16)
    dh = (dy.astype(jnp.float32) + lax.dot_general(dz, w1, nt, preferred_element_type=jnp.float32)).astype(jnp.bfloat16)
    return dh, u, dz


def _hits(ts, S, M, V):
    out = []
    for vv in range(V):
        seen = [0 <= t - S + 1 + q < V * M and V - 1 - (t - S + 1 + q) // M == vv for t in ts for q in range(S)]
        if any(seen):
            out.append((vv, all(seen)))
    return out


def _acc(d1, d2, rows, hits):
    tn = (((0,), (0,)), ((), ()))
    h, u, dz, dy = [jnp.stack([r[k] for r in rows]) for k in range(2, 6)]
    for vv, full in hits:
        hm, ym = h, dy
        if not full:
            sel = jnp.stack([r[1] & (r[0] == vv) for r in rows])[:, None, None]
            hm = jnp.where(sel, h, 0)
            ym = jnp.where(sel, dy, 0)
        d1 = d1.at[vv].add(lax.dot_general(hm.reshape(-1, hm.shape[-1]), dz.reshape(-1, dz.shape[-1]), tn, preferred_element_type=jnp.float32))
        d2 = d2.at[vv].add(lax.dot_general(u.reshape(-1, u.shape[-1]), ym.reshape(-1, ym.shape[-1]), tn, preferred_element_type=jnp.float32))
    return d1, d2


def solution(mesh):
    S = mesh.shape['stage']
    fwd_pairs = [(j, (j + 1) % S) for j in range(S)]
    bwd_pairs = [(j, (j - 1) % S) for j in range(S)]

    def body(x, g, w1, w2):
        M, B, D = x.shape
        V = w1.shape[0]
        w1 = w1[:, 0]
        w2 = w2[:, 0]
        VM = V * M
        T = VM + S - 1
        p = lax.axis_index('stage')
        first = p == 0
        last = p == S - 1
        saved = jnp.zeros((V, M, B, D), x.dtype)
        wrap = jnp.zeros((M, B, D), x.dtype)
        ybuf = jnp.zeros((M, B, D), x.dtype)
        recv = jnp.zeros((B, D), x.dtype)
        for t in range(T):
            i = t - p
            valid = (i >= 0) & (i < VM)
            ic = jnp.clip(i, 0, VM - 1)
            v, m = ic // M, ic % M
            hin = jnp.where(first, jnp.where(v == 0, x[m], wrap[m]), recv)
            saved = saved.at[v, m].set(jnp.where(valid, hin, saved[v, m]))
            hout = _fwd(hin, w1[v], w2[v])
            ybuf = ybuf.at[m].set(jnp.where(valid & last & (v == V - 1), hout, ybuf[m]))
            recv = lax.ppermute(hout, 'stage', fwd_pairs)
            j = t - (S - 1)
            if 0 <= j < VM - M:
                wrap = wrap.at[j % M].set(recv)
        dxbuf = jnp.zeros((M, B, D), x.dtype)
        d1 = jnp.zeros(w1.shape, jnp.float32)
        d2 = jnp.zeros(w2.shape, jnp.float32)
        wrapb = jnp.zeros((M, B, D), x.dtype)
        recv = jnp.zeros((B, D), x.dtype)
        rows, ts = [], []
        for t in range(T):
            i = t - (S - 1 - p)
            valid = (i >= 0) & (i < VM)
            ic = jnp.clip(i, 0, VM - 1)
            v, m = V - 1 - ic // M, ic % M
            dy = jnp.where(last, jnp.where(v == V - 1, g[m], wrapb[m]), recv)
            h = saved[v, m]
            dh, u, dz = _bwd(h, w1[v], w2[v], dy)
            rows.append((v, valid, h, u, dz, dy))
            ts.append(t)
            if len(ts) == S or t == T - 1:
                d1, d2 = _acc(d1, d2, rows, _hits(ts, S, M, V))
                rows, ts = [], []
            dxbuf = dxbuf.at[m].set(jnp.where(valid & first & (v == 0), dh, dxbuf[m]))
            recv = lax.ppermute(dh, 'stage', bwd_pairs)
            j = t - (S - 1)
            if 0 <= j < VM - M:
                wrapb = wrapb.at[j % M].set(recv)
        y = lax.psum(ybuf, 'stage')
        dx = lax.psum(dxbuf, 'stage')
        return y, dx, d1[:, None], d2[:, None]

    act = P('data', None, None)
    wsp = P(None, 'stage', None, None)
    gsp = P('data', 'stage', None, None)
    return jax.shard_map(body, mesh=mesh, in_specs=(act, act, wsp, wsp), out_specs=(act, act, gsp, gsp), check_vma=False)
```

profile of v0, /device:TPU:9, one launch (start us, length us, event | category | flops | bytes accessed | tf_op | source)
XLA Modules:
  0.0 1750.1 jit_solution(11000205320360941309)
XLA Ops:
  507.4 8.5 fusion.1455
  1093.0 9.2 fusion.60
  1112.0 9.0 fusion.4
  1121.0 11.3 scatter-add.84
  1132.3 12.8 scatter-add.66
  1158.4 13.5 bitcast_dynamic-update-slice_fusion.10
  1184.2 13.3 bitcast_dynamic-update-slice_fusion.13
  1210.2 13.7 bitcast_dynamic-update-slice_fusion.9
  1236.2 13.3 bitcast_dynamic-update-slice_fusion.12
  1261.8 10.8 bitcast_dynamic-update-slice_fusion.8
  1283.0 10.4 bitcast_dynamic-update-slice_fusion.11
  1304.1 11.0 fusion.1
  1325.4 11.2 fusion
  1346.5 10.8 fusion.3
  1367.6 10.0 fusion.2
  1377.6 15.1 copy.245
  1414.1 13.4 bitcast_dynamic-update-slice_fusion.3
  1440.0 13.2 bitcast_dynamic-update-slice_fusion.7
  1465.1 13.4 bitcast_dynamic-update-slice_fusion.2
  1490.8 13.2 bitcast_dynamic-update-slice_fusion.6
  1518.0 11.7 bitcast_dynamic-update-slice_fusion.5
  1529.7 12.3 bitcast_dynamic-update-slice_fusion.1
  1542.0 13.2 bitcast_dynamic-update-slice_fusion
  1562.2 171.6 %all-reduce.7.cloned.1.call-done = (bf16[16,256,768]{2,1,0:T(8,128)(2,1)}, bf16[16,256,768]{2,1,0:T(8,128)(2,1)}) async-done(((bf16[16,256,768]{2,1,0:T(8,128)(2,1)}, bf16[16,256,768]{2,1,0:T(8,128)(2,1)}), (bf16[16,256,768]{2,1,0:T(8,128)(2,1)}, bf16[16,256,768]{2,1,0:T(8,128)(2,1)})) %all-reduce.7.cloned.1.call-update) | async-done | bytes 12582928 | tf_op jit(solution)/shard_map/psum | solution.py:117
  (1009 shorter events, 1286.1 us)
Async XLA Ops:
  7.2 1726.7 %all-reduce.7.cloned.1.call-start = ((), (), s32[]{:S(2)}) async-start(), calls=%async_computation | async-start | bytes 25165824 | tf_op jit(solution)/shard_map/psum | solution.py:117
  20.1 16.3 collective-permute-start
  88.0 7.8 collective-permute-start.4
  623.7 7.3 collective-permute-start.33
  665.4 85.3 %collective-permute-start.34 = (bf16[256,768]{1,0:T(8,128)(2,1)S(1)}, bf16[256,768]{1,0:T(8,128)(2,1)S(1)}, u32[]{:S(2)}, u32[]{:S(2)}) collective-permute-start(bf16[256,768]{1,0:T(8,128)(2,1)S(1)} %get-tuple-element.2200), channel_id=1, source_target_pairs={{0,3},{1,0},{2,1},{3,2},{4,7},{5,4},{6,5},{7,6},{8,11},{9,8},{10,9... | collective-permute-start | bytes 1179656 | tf_op jit(solution)/shard_map/ppermute | solution.py:113
  814.7 9.1 collective-permute-start.38
  1004.3 9.2 collective-permute-start.49
  1042.7 34.8 %collective-permute-start.51 = (bf16[256,768]{1,0:T(8,128)(2,1)}, bf16[256,768]{1,0:T(8,128)(2,1)}, u32[]{:S(2)}, u32[]{:S(2)}) collective-permute-start(bf16[256,768]{1,0:T(8,128)(2,1)} %get-tuple-element.2234), channel_id=1, source_target_pairs={{0,3},{1,0},{2,1},{3,2},{4,7},{5,4},{6,5},{7,6},{8,11},{9,8},{10,9... | collective-permute-start | bytes 1179656 | tf_op jit(solution)/shard_map/ppermute | solution.py:113
  1091.4 12.0 collective-permute-start.52
  1111.4 34.7 %collective-permute-start.53 = (bf16[256,768]{1,0:T(8,128)(2,1)}, bf16[256,768]{1,0:T(8,128)(2,1)S(1)}, u32[]{:S(2)}, u32[]{:S(2)}) collective-permute-start(bf16[256,768]{1,0:T(8,128)(2,1)} %get-tuple-element.2238), channel_id=1, source_target_pairs={{0,3},{1,0},{2,1},{3,2},{4,7},{5,4},{6,5},{7,6},{8,11},{9,8},{10,9... | collective-permute-start | bytes 1179656 | tf_op jit(solution)/shard_map/ppermute | solution.py:113
  1158.1 14.8 collective-permute-start.54
  1183.7 14.9 collective-permute-start.55
  1209.4 15.6 collective-permute-start.56
  1235.7 14.8 collective-permute-start.57
  1261.5 12.2 collective-permute-start.58
  1282.5 12.0 collective-permute-start.59
  1303.3 12.9 collective-permute-start.60
  1324.8 12.9 collective-permute-start.61
  1346.4 11.9 collective-permute-start.62
  1367.0 37.7 %collective-permute-start.63 = (bf16[256,768]{1,0:T(8,128)(2,1)}, bf16[256,768]{1,0:T(8,128)(2,1)S(1)}, u32[]{:S(2)}, u32[]{:S(2)}) collective-permute-start(bf16[256,768]{1,0:T(8,128)(2,1)} %get-tuple-element.2258), channel_id=1, source_target_pairs={{0,3},{1,0},{2,1},{3,2},{4,7},{5,4},{6,5},{7,6},{8,11},{9,8},{10,9... | collective-permute-start | bytes 1179656 | tf_op jit(solution)/shard_map/ppermute | solution.py:113
  1413.3 15.2 collective-permute-start.64
  1439.2 15.0 collective-permute-start.65
  1465.1 14.4 collective-permute-start.66
  1490.3 14.8 collective-permute-start.67
  (258 other events, 2092.2 us)
Sparse Core Ops, SparseCore 0:
  1517.1 216.6 all-reduce.6
where the time goes:
time: 1770 us; the launch traced here: 1750 us
  matrix products  895 us (51%)
  waiting for transfers between devices  260 us (15%)
  local copies, waits for them, and re-layouts  251 us (14%)
  other arithmetic  232 us (13%)
  starting transfers between devices  94.5 us (5%)
  between operations  18.1 us (1%)
    dot_general x35, matrix products, _fwd(): r = jnp.dot(u, w2, preferred_element_type=jnp.float32)  283 us
    dot_general x35, matrix products, _bwd(): du = lax.dot_general(dy, w2, nt, preferred_element_type=jnp.float32)  181 us
    psum x1, waiting for transfers between devices, body(): y = lax.psum(ybuf, 'stage')  172 us
    dot_general x10, matrix products, _acc(): lax.dot_general(u.reshape(-1, u.shape[-1]), ym.reshape(-1, ym.shape[-1]),...  122 us
    dot_general x35, matrix products, _bwd(): lax.dot_general(dz, w1, nt, preferred_element_type=jnp.float32)  116 us
    dot_general x10, matrix products, _acc(): lax.dot_general(hm.reshape(-1, hm.shape[-1]), dz.reshape(-1, dz.shape[-1]...  112 us
    scatter x35, other arithmetic, body(): saved = saved.at[v, m].set(jnp.where(valid, hin, saved[v, m]))  94.3 us
    dot_general x35, matrix products, _bwd(): z = jnp.dot(h, w1, preferred_element_type=jnp.float32)  81.7 us
  transfers between devices with their start and end apart: 69, of which 45 were waited for; matrix products, arithmetic and copies ran while one was open for 35% of the time, Pallas kernels for 0%

commit v1 on v0

v1 whole, which is shorter than its diff:
```python
import functools

import jax
import jax.numpy as jnp
from jax import lax
from jax.experimental import pallas as pl
from jax.experimental.pallas import tpu as pltpu
from jax.sharding import PartitionSpec as P

BF = jnp.bfloat16
F32 = jnp.float32
MESH = pl.DeviceIdType.MESH
NT = (((1,), (1,)), ((), ()))
GROUP = 8
LEAD = 9
STEP = 3


def _gelu(z):
    return 0.5 * z * (1.0 + lax.erf(z * 0.7071067811865476))


def _gelu_pair(z):
    half = 0.5 * (1.0 + lax.erf(z * 0.7071067811865476))
    return z * half, half + z * jnp.exp(-0.5 * z * z) * 0.3989422804014327


def _dot(a, b):
    return jnp.dot(a, b, preferred_element_type=F32)


def _dot_nt(a, b):
    return lax.dot_general(a, b, NT, preferred_element_type=F32)


def _pipeline(S, V, M, G, x, g, w1_hbm, w2_hbm, u_out, dz_out, h_out, dy_out, r_out,
              w1, w2, hbuf, dybuf, us, ub, dzb, fo, bo,
              f_recv, b_recv, f_send, b_send, h_sem, dy_sem, u_sem, dz_sem, w_sem):
    p = lax.axis_index('stage')
    nxt = lax.rem(p + 1, S)
    prv = lax.rem(p + S - 1, S)
    first = p == 0
    last = p == S - 1
    n = V * M
    F = w1.shape[-1]
    chunk = 256 if F % 256 == 0 else F

    barrier = pltpu.get_barrier_semaphore()
    for q in (prv, nxt):
        pl.semaphore_signal(barrier, inc=1, device_id={'stage': q}, device_id_type=MESH)

    def load_w(v):
        pltpu.make_async_copy(w1_hbm.at[v], w1.at[v], w_sem.at[2 * v]).start()
        pltpu.make_async_copy(w2_hbm.at[v], w2.at[v], w_sem.at[2 * v + 1]).start()

    def wait_w(v):
        pltpu.make_async_copy(w1_hbm.at[v], w1.at[v], w_sem.at[2 * v]).wait()
        pltpu.make_async_copy(w2_hbm.at[v], w2.at[v], w_sem.at[2 * v + 1]).wait()

    def load_x(m):
        pltpu.make_async_copy(x.at[m], hbuf.at[m], f_recv.at[m]).start()

    def load_g(m):
        s = (V - 1) * M + m
        pltpu.make_async_copy(g.at[m], dybuf.at[s], b_recv.at[s]).start()

    @pl.when(first)
    def _():
        load_x(0)

    load_w(0)

    @pl.when(first)
    def _():
        lax.fori_loop(1, M, lambda m, c: (load_x(m), c)[1], 0)

    for v in range(1, V):
        load_w(v)

    @pl.when(last)
    def _():
        lax.fori_loop(0, M, lambda m, c: (load_g(m), c)[1], 0)

    pl.semaphore_wait(barrier, 2)
    wait_w(0)

    def place(i):
        blk, r = i // (V * G), lax.rem(i, V * G)
        return r // G, blk * G + lax.rem(r, G)

    def wait_f_send(s):
        pltpu.make_async_copy(fo.at[s], r_out.at[0], f_send.at[s]).wait()

    def wait_b_send(s):
        pltpu.make_async_copy(bo.at[s], r_out.at[0], b_send.at[s]).wait()

    def wait_uz(s):
        pltpu.make_async_copy(ub.at[s], u_out.at[0], u_sem.at[s]).wait()
        pltpu.make_async_copy(dzb.at[s], dz_out.at[0], dz_sem.at[s]).wait()

    def forward(i):
        v, m = place(i)
        slot = v * M + m
        s = lax.rem(i, 2)
        for vv in range(1, V):
            @pl.when(i == vv * G)
            def _():
                wait_w(vv)
        pltpu.make_async_copy(fo.at[0], hbuf.at[slot], f_recv.at[slot]).wait()
        pltpu.make_async_copy(hbuf.at[slot], h_out.at[slot], h_sem.at[slot]).start()

        @pl.when(i >= 2)
        def _():
            wait_f_send(s)

        for c in range(F // chunk):
            cs = slice(c * chunk, (c + 1) * chunk)
            us[:, cs] = _gelu(_dot(hbuf[slot], w1[v, :, cs])).astype(BF)
        fo[s] = (hbuf[slot].astype(F32) + _dot(us[...], w2[v])).astype(BF)

        final = last & (v == V - 1)

        @pl.when(final)
        def _():
            pltpu.make_async_copy(fo.at[s], r_out.at[m], f_send.at[s]).start()

        @pl.when(jnp.logical_not(final))
        def _():
            to = slot + jnp.where(last, M, 0)
            pltpu.make_async_remote_copy(
                src_ref=fo.at[s], dst_ref=hbuf.at[to], send_sem=f_send.at[s], recv_sem=f_recv.at[to],
                device_id={'stage': nxt}, device_id_type=MESH).start()

    def backward(j):
        vr, m = place(j)
        v = V - 1 - vr
        slot = v * M + m
        s = lax.rem(j, 2)
        pltpu.make_async_copy(bo.at[0], dybuf.at[slot], b_recv.at[slot]).wait()
        pltpu.make_async_copy(dybuf.at[slot], dy_out.at[slot], dy_sem.at[slot]).start()

        @pl.when(j >= 2)
        def _():
            wait_b_send(s)
            wait_uz(s)

        for c in range(F // chunk):
            cs = slice(c * chunk, (c + 1) * chunk)
            a, b = _gelu_pair(_dot(hbuf[slot], w1[v, :, cs]))
            ub[s, :, cs] = a.astype(BF)
            dzb[s, :, cs] = (_dot_nt(dybuf[slot], w2[v, cs, :]) * b).astype(BF)
        pltpu.make_async_copy(ub.at[s], u_out.at[slot], u_sem.at[s]).start()
        bo[s] = (dybuf[slot].astype(F32) + _dot_nt(dzb[s], w1[v])).astype(BF)
        pltpu.make_async_copy(dzb.at[s], dz_out.at[slot], dz_sem.at[s]).start()

        final = first & (v == 0)

        @pl.when(final)
        def _():
            pltpu.make_async_copy(bo.at[s], r_out.at[m], b_send.at[s]).start()

        @pl.when(jnp.logical_not(final))
        def _():
            to = slot - jnp.where(first, M, 0)
            pltpu.make_async_remote_copy(
                src_ref=bo.at[s], dst_ref=dybuf.at[to], send_sem=b_send.at[s], recv_sem=b_recv.at[to],
                device_id={'stage': prv}, device_id_type=MESH).start()

    lead = LEAD * G // GROUP + STEP * (S - 1 - p)

    def step(k, carry):
        @pl.when(k < n)
        def _():
            forward(k)

        @pl.when(k >= lead)
        def _():
            backward(k - lead)

        return carry

    lax.fori_loop(0, n + lead, step, 0)

    for s in range(2):
        wait_f_send(s)
        wait_b_send(s)
        wait_uz(s)

    def drain(slot, carry):
        pltpu.make_async_copy(hbuf.at[slot], h_out.at[slot], h_sem.at[slot]).wait()
        pltpu.make_async_copy(dybuf.at[slot], dy_out.at[slot], dy_sem.at[slot]).wait()
        return carry

    lax.fori_loop(0, n, drain, 0)


def solution(mesh):
    S = mesh.shape['stage']

    def body(x, g, w1, w2):
        M, B, D = x.shape
        V, _, _, F = w1.shape
        w1 = w1[:, 0]
        w2 = w2[:, 0]
        G = min(GROUP, M)
        n = V * M
        p = lax.axis_index('stage')
        anys = pl.BlockSpec(memory_space=pl.ANY)
        dma = pltpu.SemaphoreType.DMA
        u, dz, h, dy, r = pl.pallas_call(
            functools.partial(_pipeline, S, V, M, G),
            out_shape=[
                jax.ShapeDtypeStruct((n, B, F), BF),
                jax.ShapeDtypeStruct((n, B, F), BF),
                jax.ShapeDtypeStruct((n, B, D), BF),
                jax.ShapeDtypeStruct((n, B, D), BF),
                jax.ShapeDtypeStruct((M, B, D), BF),
            ],
            in_specs=[anys] * 4,
            out_specs=[anys] * 5,
            scratch_shapes=[
                pltpu.VMEM((V, D, F), BF),
                pltpu.VMEM((V, F, D), BF),
                pltpu.VMEM((n, B, D), BF),
                pltpu.VMEM((n, B, D), BF),
                pltpu.VMEM((B, F), BF),
                pltpu.VMEM((2, B, F), BF),
                pltpu.VMEM((2, B, F), BF),
                pltpu.VMEM((2, B, D), BF),
                pltpu.VMEM((2, B, D), BF),
                dma((n,)), dma((n,)), dma((2,)), dma((2,)),
                dma((n,)), dma((n,)), dma((2,)), dma((2,)), dma((2 * V,)),
            ],
            compiler_params=pltpu.CompilerParams(
                collective_id=0, has_side_effects=True, vmem_limit_bytes=62 * 2 ** 20),
            cost_estimate=pl.CostEstimate(
                flops=10 * n * B * D * F, bytes_accessed=4 * n * B * F, transcendentals=3 * n * B * F),
            name='pipeline',
        )(x, g, w1, w2)

        tn = (((1,), (1,)), ((0,), (0,)))
        h = h.reshape(V, M * B, D)
        dz = dz.reshape(V, M * B, F)
        u = u.reshape(V, M * B, F)
        dy = dy.reshape(V, M * B, D)
        d1 = lax.dot_general(h, dz, tn, preferred_element_type=F32)
        d2 = lax.dot_general(u, dy, tn, preferred_element_type=F32)

        if S == 4:
            near = lax.ppermute(r, 'stage', [(0, 1), (3, 2)])
            far = lax.ppermute(r, 'stage', [(0, 2), (3, 1)])
            back = lax.ppermute(far, 'stage', [(1, 0), (2, 3)])
            y = jnp.where(p == 0, back, jnp.where(p == 1, far, jnp.where(p == 2, near, r)))
            dx = jnp.where(p == 0, r, jnp.where(p == 1, near, jnp.where(p == 2, far, back)))
        return y, dx, d1[:, None], d2[:, None]

    act = P('data', None, None)
    wsp = P(None, 'stage', None, None)
    gsp = P('data', 'stage', None, None)
    return jax.shard_map(body, mesh=mesh, in_specs=(act, act, wsp, wsp), out_specs=(act, act, gsp, gsp), check_vma=False)
```

time: 1770 us -> 482 us (0.27); the launches traced: 1750 us -> 482 us
  matrix products: 895 us -> 97.3 us
  Pallas kernels: 0 us -> 290 us
  local copies, waits for them, and re-layouts: 251 us -> 0 us
  other arithmetic: 232 us -> 14.1 us
  waiting for transfers between devices: 260 us -> 69.1 us
  starting transfers between devices: 94.5 us -> 10.3 us
    dot_general x160 -> x2, matrix products: 895 us -> 97.3 us  [the longest x1 48.7 us: body(): d1 = lax.dot_general(h, dz, tn, preferred_element_type=F32)]
    pallas_call x0 -> x1, Pallas kernels: none -> 290 us  [body(): pl.pallas_call(functools.partial(_pipeline, S, V, M, G), out_shape=[jax.S...]
    psum x1 -> x0, waiting for transfers between devices: 172 us -> none  [body(): y = lax.psum(ybuf, 'stage')]
    dynamic_slice x102 -> x0, local copies, waits for them, and re-layouts: 109 us -> none  [the longest x34 38.2 us: body(): dxbuf = dxbuf.at[m].set(jnp.where(valid & first & (v == 0), dh, dxbuf[m]))]
    another operation x58 -> x0, other arithmetic: 95.4 us -> none  [the longest x18 63.9 us: _acc(): h, u, dz, dy = [jnp.stack([r[k] for r in rows]) for k in range(2, 6)]]
    scatter x35 -> x0, other arithmetic: 94.3 us -> none  [body(): saved = saved.at[v, m].set(jnp.where(valid, hin, saved[v, m]))]
    ppermute x68 -> x3, starting transfers between devices: 94.5 us -> 10.3 us  [the longest x1 7.69 us: body(): back = lax.ppermute(far, 'stage', [(1, 0), (2, 3)])]
    another operation x30 -> x0, local copies, waits for them, and re-layouts: 43.5 us -> none  [the longest x28 36.4 us: _acc(): h, u, dz, dy = [jnp.stack([r[k] for r in rows]) for k in range(2, 6)]]
  transfers between devices with their start and end apart: 69 -> 3, of which waited for: 45 -> 1; matrix products, arithmetic and copies ran while one was open for 35% -> 20% of each run, Pallas kernels for 0% -> 0%
where the time goes in v1:
time: 482 us
  Pallas kernels  290 us (60%)
  matrix products  97.3 us (20%)
  waiting for transfers between devices  69.1 us (14%)
  other arithmetic  14.1 us (3%)
  starting transfers between devices  10.3 us (2%)
    pallas_call x1, Pallas kernels, body(): pl.pallas_call(functools.partial(_pipeline, S, V, M, G), out_shape=[jax.S...  290 us
    ppermute x1, waiting for transfers between devices, body(): far = lax.ppermute(r, 'stage', [(0, 2), (3, 1)])  69.1 us
    dot_general x1, matrix products, body(): d1 = lax.dot_general(h, dz, tn, preferred_element_type=F32)  48.7 us
    dot_general x1, matrix products, body(): d2 = lax.dot_general(u, dy, tn, preferred_element_type=F32)  48.5 us
    select_n x1, other arithmetic, body(): jnp.where(p == 0, r, jnp.where(p == 1, near, jnp.where(p == 2, far, back)))  14.1 us
  transfers between devices with their start and end apart: 3, of which 1 were waited for; matrix products, arithmetic and copies ran while one was open for 20% of the time, Pallas kernels for 0%

profile of v1, /device:TPU:9, one launch (start us, length us, event | category | flops | bytes accessed | tf_op | source)
XLA Modules:
  0.0 481.7 jit_solution(12390453438779171805)
XLA Ops:
  0.6 290.3 %pipeline.1 = (bf16[32,256,3072]{2,1,0:T(8,128)(2,1)}, bf16[32,256,3072]{2,1,0:T(8,128)(2,1)}, bf16[32,256,768]{2,1,0:T(8,128)(2,1)}, bf16[32,256,768]{2,1,0:T(8,128)(2,1)}, bf16[16,256,768]{2,1,0:T(8,128)(2,1)}) custom-call(bf16[16,256,768]{2,1,0:T(8,128)(2,1)} %x.1, bf16[16,256,768]{2,1,0:T(8,128)(2,1)} %g.1, bf16[2,768,3072]{2,1,0:T(8,128)(2,1)} %bitcast.18, ...), custom_call_target="tpu_custom_call" | custom-call | flops 193273528320 | bytes 100663296 | tf_op jit(solution)/shard_map/pipeline/pallas_call | solution.py:210
  290.9 1.3 collective-permute-start
  292.2 1.3 collective-permute-start.2
  293.5 69.1 %collective-permute-done = bf16[16,256,768]{2,1,0:T(8,128)(2,1)} collective-permute-done((bf16[16,256,768]{2,1,0:T(8,128)(2,1)}, bf16[16,256,768]{2,1,0:T(8,128)(2,1)}, u32[]{:S(2)}, u32[]{:S(2)}) %collective-permute-start) | collective-permute-done | bytes 6291488 | tf_op jit(solution)/shard_map/ppermute | solution.py:251
  362.7 7.7 %collective-permute-start.1 = (bf16[16,256,768]{2,1,0:T(8,128)(2,1)}, bf16[16,256,768]{2,1,0:T(8,128)(2,1)}, u32[]{:S(2)}, u32[]{:S(2)}) collective-permute-start(bf16[16,256,768]{2,1,0:T(8,128)(2,1)} %collective-permute-done), channel_id=1, source_target_pairs={{1,0},{2,3},{5,4},{6,7},{9,8},{10,11},{13,12},{14,15}} | collective-permute-start | bytes 18874376 | tf_op jit(solution)/shard_map/ppermute | solution.py:252
  370.4 48.5 %convolution_bitcast_fusion.1 = f32[2,1,3072,768]{3,2,1,0:T(8,128)} fusion(bf16[2,4096,3072]{2,1,0:T(8,128)(2,1)} %bitcast.21, bf16[2,4096,768]{2,1,0:T(8,128)(2,1)} %bitcast.23), kind=kOutput, calls=%fused_computation.1 | convolution fusion | flops 38654705664 | bytes 81788928 | tf_op jit(solution)/shard_map/dot_general | solution.py:247
  418.9 48.7 %convolution_bitcast_fusion = f32[2,1,768,3072]{3,2,1,0:T(8,128)} fusion(bf16[2,4096,768]{2,1,0:T(8,128)(2,1)} %bitcast.22, bf16[2,4096,3072]{2,1,0:T(8,128)(2,1)} %bitcast.20), kind=kOutput, calls=%fused_computation | convolution fusion | flops 38654705664 | bytes 81788928 | tf_op jit(solution)/shard_map/dot_general | solution.py:246
  467.6 0.0 collective-permute-done.2
  467.6 0.0 collective-permute-done.1
  467.6 14.1 %select_select_fusion = (bf16[16,256,768]{2,1,0:T(8,128)(2,1)}, bf16[16,256,768]{2,1,0:T(8,128)(2,1)}) fusion(bf16[16,256,768]{2,1,0:T(8,128)(2,1)} %get-tuple-element.9, bf16[16,256,768]{2,1,0:T(8,128)(2,1)} %collective-permute-done.2, bf16[16,256,768]{2,1,0:T(8,128)(2,1)} %collective-permute-done, bf16[16,256,768]{2,1,0:T(8,128)(2,1)} %collective-permute-done.1, ...), kind=kLoop, calls=%fused_computation.2 | loop fusion | flops 18874368 | bytes 37748740 | tf_op jit(solution)/shard_map/jit(_where)/select_n | solution.py:254
Async XLA Ops:
  290.9 71.7 %collective-permute-start = (bf16[16,256,768]{2,1,0:T(8,128)(2,1)}, bf16[16,256,768]{2,1,0:T(8,128)(2,1)}, u32[]{:S(2)}, u32[]{:S(2)}) collective-permute-start(bf16[16,256,768]{2,1,0:T(8,128)(2,1)} %get-tuple-element.9), channel_id=1, source_target_pairs={{0,2},{3,1},{4,6},{7,5},{8,10},{11,9},{12,14},{15,13}} | collective-permute-start | bytes 18874376 | tf_op jit(solution)/shard_map/ppermute | solution.py:251
  292.2 175.4 %collective-permute-start.2 = (bf16[16,256,768]{2,1,0:T(8,128)(2,1)}, bf16[16,256,768]{2,1,0:T(8,128)(2,1)}, u32[]{:S(2)}, u32[]{:S(2)}) collective-permute-start(bf16[16,256,768]{2,1,0:T(8,128)(2,1)} %get-tuple-element.9), channel_id=1, source_target_pairs={{0,1},{3,2},{4,5},{7,6},{8,9},{11,10},{12,13},{15,14}} | collective-permute-start | bytes 18874376 | tf_op jit(solution)/shard_map/ppermute | solution.py:250
  362.7 105.0 %collective-permute-start.1 = (bf16[16,256,768]{2,1,0:T(8,128)(2,1)}, bf16[16,256,768]{2,1,0:T(8,128)(2,1)}, u32[]{:S(2)}, u32[]{:S(2)}) collective-permute-start(bf16[16,256,768]{2,1,0:T(8,128)(2,1)} %collective-permute-done), channel_id=1, source_target_pairs={{1,0},{2,3},{5,4},{6,7},{9,8},{10,11},{13,12},{14,15}} | collective-permute-start | bytes 18874376 | tf_op jit(solution)/shard_map/ppermute | solution.py:252

commit v2 on v1

--- a/solution.py
+++ b/solution.py
@@ -12,8 +12,13 @@
 MESH = pl.DeviceIdType.MESH
 NT = (((1,), (1,)), ((), ()))
 GROUP = 8
-LEAD = 9
-STEP = 3
+ORDER = (
+    'FFFFFFFFFFFFFFFFFFFFFFFBFBBBBFBFBFBFBFBFBFBFBBBBBBBBBBBBBBBBBBBB',
+    'FFFFFFFFFFFFFFFFFFFBFBFBFBFBFBBFBFBFBFBFBFBFBFBBBBBBBBBBBBBBBBBB',
+    'FFFFFFFFFFFBFFBFBFBFBFBFBFBFBFBFBFBFBFBFBFBFBFBFBFBFBBBBBBBBBBBB',
+    'FFFFFFFFBBBFBBFBFBFBBFFFBFBFBFBFBFBFBBFBFBFBFBFBFBFBBBBBFBBBBFFF',
+)
+WORD = 16
 
 
 def _gelu(z):
@@ -33,15 +38,22 @@
     return lax.dot_general(a, b, NT, preferred_element_type=F32)
 
 
-def _pipeline(S, V, M, G, x, g, w1_hbm, w2_hbm, u_out, dz_out, h_out, dy_out, r_out,
+def _words(row):
+    return [sum((c == 'B') << b for b, c in enumerate(row[k:k + WORD])) for k in range(0, len(row), WORD)]
+
+
+def _pipeline(S, V, M, G, x, g, w1_hbm, w2_hbm, u_out, dz_out, h_out, dy_out, mine, other,
               w1, w2, hbuf, dybuf, us, ub, dzb, fo, bo,
-              f_recv, b_recv, f_send, b_send, h_sem, dy_sem, u_sem, dz_sem, w_sem):
+              f_recv, b_recv, f_send, b_send, h_sem, dy_sem, u_sem, dz_sem, w_sem, pair_send, pair_recv):
     p = lax.axis_index('stage')
     nxt = lax.rem(p + 1, S)
     prv = lax.rem(p + S - 1, S)
+    parity = lax.rem(p, 2)
+    partner = p + 1 - 2 * parity
     first = p == 0
     last = p == S - 1
     n = V * M
+    H = M // 2
     F = w1.shape[-1]
     chunk = 256 if F % 256 == 0 else F
 
@@ -88,41 +100,83 @@
         blk, r = i // (V * G), lax.rem(i, V * G)
         return r // G, blk * G + lax.rem(r, G)
 
-    def wait_f_send(s):
-        pltpu.make_async_copy(fo.at[s], r_out.at[0], f_send.at[s]).wait()
-
-    def wait_b_send(s):
-        pltpu.make_async_copy(bo.at[s], r_out.at[0], b_send.at[s]).wait()
+    def place_f(i):
+        v, m = place(i)
+        early = i < G + G // 2
+        v = jnp.where(last, jnp.where(i < G, 0, jnp.where(early, 1, jnp.where(i < 2 * G + G // 2, 0, 1))), v)
+        m = jnp.where(last, jnp.where(i < G, i, jnp.where(early, i - G, jnp.where(i < 2 * G + G // 2, i - G // 2, i - 2 * G))), m)
+        return v, m
+
+    def wait_f_send(i):
+        s = lax.rem(i, 2)
+        pltpu.make_async_copy(fo.at[s], mine.at[0], f_send.at[s]).wait()
+
+        @pl.when(last & (place_f(i)[0] == V - 1))
+        def _():
+            pltpu.make_async_copy(fo.at[s], mine.at[0], pair_send.at[s]).wait()
+
+    def wait_b_send(j):
+        s = lax.rem(j, 2)
+        pltpu.make_async_copy(bo.at[s], mine.at[0], b_send.at[s]).wait()
+
+        @pl.when(first & (place(j)[0] == V - 1))
+        def _():
+            pltpu.make_async_copy(bo.at[s], mine.at[0], pair_send.at[s]).wait()
 
     def wait_uz(s):
         pltpu.make_async_copy(ub.at[s], u_out.at[0], u_sem.at[s]).wait()
         pltpu.make_async_copy(dzb.at[s], dz_out.at[0], dz_sem.at[s]).wait()
 
+    def take_h(slot):
+        pltpu.make_async_copy(fo.at[0], hbuf.at[slot], f_recv.at[slot]).wait()
+        pltpu.make_async_copy(hbuf.at[slot], h_out.at[slot], h_sem.at[slot]).start()
+
+    def finish(src, s, m, sem):
+        k = lax.rem(m, H)
+        upper = m // H
+        own = upper == parity
+
+        def send(here, there):
+            pltpu.make_async_copy(src.at[s], here.at[k], sem.at[s]).start()
+            pltpu.make_async_remote_copy(
+                src_ref=src.at[s], dst_ref=there.at[k], send_sem=pair_send.at[s], recv_sem=pair_recv.at[m],
+                device_id={'stage': partner}, device_id_type=MESH).start()
+
+        @pl.when(own)
+        def _():
+            send(mine, other)
+
+        @pl.when(jnp.logical_not(own))
+        def _():
+            send(other, mine)
+
     def forward(i):
-        v, m = place(i)
+        v, m = place_f(i)
         slot = v * M + m
         s = lax.rem(i, 2)
-        for vv in range(1, V):
-            @pl.when(i == vv * G)
-            def _():
+        final = last & (v == V - 1)
+
+        @pl.when(i == G - 1)
+        def _():
+            for vv in range(1, V):
                 wait_w(vv)
-        pltpu.make_async_copy(fo.at[0], hbuf.at[slot], f_recv.at[slot]).wait()
-        pltpu.make_async_copy(hbuf.at[slot], h_out.at[slot], h_sem.at[slot]).start()
+
+        @pl.when(jnp.logical_not(final))
+        def _():
+            take_h(slot)
 
         @pl.when(i >= 2)
         def _():
-            wait_f_send(s)
+            wait_f_send(i - 2)
 
         for c in range(F // chunk):
             cs = slice(c * chunk, (c + 1) * chunk)
             us[:, cs] = _gelu(_dot(hbuf[slot], w1[v, :, cs])).astype(BF)
         fo[s] = (hbuf[slot].astype(F32) + _dot(us[...], w2[v])).astype(BF)
 
-        final = last & (v == V - 1)
-
         @pl.when(final)
         def _():
-            pltpu.make_async_copy(fo.at[s], r_out.at[m], f_send.at[s]).start()
+            finish(fo, s, m, f_send)
 
         @pl.when(jnp.logical_not(final))
         def _():
@@ -136,12 +190,17 @@
         v = V - 1 - vr
         slot = v * M + m
         s = lax.rem(j, 2)
+
+        @pl.when(last & (v == V - 1))
+        def _():
+            take_h(slot)
+
         pltpu.make_async_copy(bo.at[0], dybuf.at[slot], b_recv.at[slot]).wait()
         pltpu.make_async_copy(dybuf.at[slot], dy_out.at[slot], dy_sem.at[slot]).start()
 
         @pl.when(j >= 2)
         def _():
-            wait_b_send(s)
+            wait_b_send(j - 2)
             wait_uz(s)
 
         for c in range(F // chunk):
@@ -157,7 +216,7 @@
 
         @pl.when(final)
         def _():
-            pltpu.make_async_copy(bo.at[s], r_out.at[m], b_send.at[s]).start()
+            finish(bo, s, m, b_send)
 
         @pl.when(jnp.logical_not(final))
         def _():
@@ -166,25 +225,37 @@
                 src_ref=bo.at[s], dst_ref=dybuf.at[to], send_sem=b_send.at[s], recv_sem=b_recv.at[to],
                 device_id={'stage': prv}, device_id_type=MESH).start()
 
-    lead = LEAD * G // GROUP + STEP * (S - 1 - p)
-
-    def step(k, carry):
-        @pl.when(k < n)
-        def _():
-            forward(k)
-
-        @pl.when(k >= lead)
-        def _():
-            backward(k - lead)
-
-        return carry
-
-    lax.fori_loop(0, n + lead, step, 0)
-
-    for s in range(2):
-        wait_f_send(s)
-        wait_b_send(s)
-        wait_uz(s)
+    table = [_words(row) for row in ORDER]
+
+    def word(k):
+        out = jnp.int32(0)
+        for q in range(S):
+            for b in range(2 * n // WORD):
+                out = jnp.where((p == q) & (k == b), table[q][b], out)
+        return out
+
+    def step(t, carry):
+        i, j, bits = carry
+        bits = jnp.where(lax.rem(t, WORD) == 0, word(t // WORD), bits)
+        back = lax.rem(bits, 2)
+
+        @pl.when(back == 0)
+        def _():
+            forward(i)
+
+        @pl.when(back == 1)
+        def _():
+            backward(j)
+
+        return i + 1 - back, j + back, bits // 2
+
+    zero = jnp.int32(0)
+    lax.fori_loop(0, 2 * n, step, (zero, zero, zero))
+
+    for k in (n - 2, n - 1):
+        wait_f_send(jnp.int32(k))
+        wait_b_send(jnp.int32(k))
+        wait_uz(k % 2)
 
     def drain(slot, carry):
         pltpu.make_async_copy(hbuf.at[slot], h_out.at[slot], h_sem.at[slot]).wait()
@@ -192,6 +263,72 @@
         return carry
 
     lax.fori_loop(0, n, drain, 0)
+
+    @pl.when(jnp.logical_not(first | last))
+    def _():
+        lax.fori_loop(
+            0, M, lambda m, c: (pltpu.make_async_copy(fo.at[0], mine.at[0], pair_recv.at[m]).wait(), c)[1], 0)
+
+
+def _grad_kernel(a, b, *rest):
+    rest[-1][0] = lax.dot_general(a[0], b[0], (((0,), (0,)), ((), ())), preferred_element_type=F32)
+
+
+def _grad(name, a, b, wide, layers, into=None):
+    V, T, A = a.shape
+    N = b.shape[-1]
+    lo, cnt = layers
+    block = 512 if max(A, N) % 512 == 0 else max(A, N)
+    nb = (A if wide == 0 else N) // block
+    if wide == 0:
+        specs = [pl.BlockSpec((1, T, block), lambda v, i: (v + lo, 0, i)), pl.BlockSpec((1, T, N), lambda v, i: (v + lo, 0, 0))]
+        out = pl.BlockSpec((1, block, N), lambda v, i: (v + lo, i, 0))
+    else:
+        specs = [pl.BlockSpec((1, T, A), lambda v, i: (v + lo, 0, 0)), pl.BlockSpec((1, T, block), lambda v, i: (v + lo, 0, i))]
+        out = pl.BlockSpec((1, A, block), lambda v, i: (v + lo, 0, i))
+    args = [a, b]
+    alias = {}
+    if into is not None:
+        args.append(into)
+        specs.append(pl.BlockSpec(memory_space=pl.ANY))
+        alias = {2: 0}
+    return pl.pallas_call(
+        _grad_kernel,
+        grid=(cnt, nb),
+        out_shape=jax.ShapeDtypeStruct((V, A, N), F32),
+        in_specs=specs,
+        out_specs=out,
+        input_output_aliases=alias,
+        compiler_params=pltpu.CompilerParams(vmem_limit_bytes=48 * 2 ** 20),
+        cost_estimate=pl.CostEstimate(
+            flops=2 * cnt * T * A * N, bytes_accessed=cnt * (2 * T * (A + N) + 4 * A * N), transcendentals=0),
+        name=name,
+    )(*args)
+
+
+def _assemble(S, M, mine, other, far, back, y, dx, sem):
+    p = lax.axis_index('stage')
+    parity = lax.rem(p, 2)
+    left = p < S // 2
+    H = M // 2
+
+    def put(src, k, dst, upper):
+        pltpu.make_async_copy(src, dst.at[pl.ds(upper * H, H)], sem.at[k]).start()
+
+    for k, src in enumerate((mine, other, far, back)):
+        upper = parity if k % 2 == 0 else 1 - parity
+        to_dx = left if k < 2 else jnp.logical_not(left)
+
+        @pl.when(to_dx)
+        def _():
+            put(src, k, dx, upper)
+
+        @pl.when(jnp.logical_not(to_dx))
+        def _():
+            put(src, k, y, upper)
+
+    for k in range(4):
+        pltpu.make_async_copy(mine, y.at[pl.ds(0, H)], sem.at[k]).wait()
 
 
 def solution(mesh):
@@ -202,22 +339,22 @@
         V, _, _, F = w1.shape
         w1 = w1[:, 0]
         w2 = w2[:, 0]
-        G = min(GROUP, M)
+        G = GROUP
         n = V * M
-        p = lax.axis_index('stage')
         anys = pl.BlockSpec(memory_space=pl.ANY)
         dma = pltpu.SemaphoreType.DMA
-        u, dz, h, dy, r = pl.pallas_call(
+        half = jax.ShapeDtypeStruct((M // 2, B, D), BF)
+        u, dz, h, dy, mine, other = pl.pallas_call(
             functools.partial(_pipeline, S, V, M, G),
             out_shape=[
                 jax.ShapeDtypeStruct((n, B, F), BF),
                 jax.ShapeDtypeStruct((n, B, F), BF),
                 jax.ShapeDtypeStruct((n, B, D), BF),
                 jax.ShapeDtypeStruct((n, B, D), BF),
-                jax.ShapeDtypeStruct((M, B, D), BF),
+                half, half,
             ],
             in_specs=[anys] * 4,
-            out_specs=[anys] * 5,
+            out_specs=[anys] * 6,
             scratch_shapes=[
                 pltpu.VMEM((V, D, F), BF),
                 pltpu.VMEM((V, F, D), BF),
@@ -229,7 +366,7 @@
                 pltpu.VMEM((2, B, D), BF),
                 pltpu.VMEM((2, B, D), BF),
                 dma((n,)), dma((n,)), dma((2,)), dma((2,)),
-                dma((n,)), dma((n,)), dma((2,)), dma((2,)), dma((2 * V,)),
+                dma((n,)), dma((n,)), dma((2,)), dma((2,)), dma((2 * V,)), dma((2,)), dma((M,)),
             ],
             compiler_params=pltpu.CompilerParams(
                 collective_id=0, has_side_effects=True, vmem_limit_bytes=62 * 2 ** 20),
@@ -238,20 +375,28 @@
             name='pipeline',
         )(x, g, w1, w2)
 
-        tn = (((1,), (1,)), ((0,), (0,)))
         h = h.reshape(V, M * B, D)
         dz = dz.reshape(V, M * B, F)
         u = u.reshape(V, M * B, F)
         dy = dy.reshape(V, M * B, D)
-        d1 = lax.dot_general(h, dz, tn, preferred_element_type=F32)
-        d2 = lax.dot_general(u, dy, tn, preferred_element_type=F32)
-
-        if S == 4:
-            near = lax.ppermute(r, 'stage', [(0, 1), (3, 2)])
-            far = lax.ppermute(r, 'stage', [(0, 2), (3, 1)])
-            back = lax.ppermute(far, 'stage', [(1, 0), (2, 3)])
-            y = jnp.where(p == 0, back, jnp.where(p == 1, far, jnp.where(p == 2, near, r)))
-            dx = jnp.where(p == 0, r, jnp.where(p == 1, near, jnp.where(p == 2, far, back)))
+
+        far = lax.ppermute(mine, 'stage', [(q, (q + S // 2) % S) for q in range(S)])
+        d1 = _grad('grad1', h, dz, 1, (0, V))
+        d2 = _grad('grad2', u, dy, 0, (0, V - 1))
+        far, d1, d2 = lax.optimization_barrier((far, d1, d2))
+        back = lax.ppermute(far, 'stage', [(q, q + 1 - 2 * (q % 2)) for q in range(S)])
+        d2 = _grad('grad3', u, dy, 0, (V - 1, 1), d2)
+        back, d2 = lax.optimization_barrier((back, d2))
+        full = jax.ShapeDtypeStruct((M, B, D), BF)
+        y, dx = pl.pallas_call(
+            functools.partial(_assemble, S, M),
+            out_shape=[full, full],
+            in_specs=[pl.BlockSpec(memory_space=pltpu.VMEM)] * 4,
+            out_specs=[anys] * 2,
+            scratch_shapes=[dma((4,))],
+            compiler_params=pltpu.CompilerParams(vmem_limit_bytes=16 * 2 ** 20),
+            name='assemble',
+        )(mine, other, far, back)
         return y, dx, d1[:, None], d2[:, None]
 
     act = P('data', None, None)

time: 482 us -> 400 us (0.83)
  Pallas kernels: 290 us -> 398 us
  matrix products: 97.3 us -> 0 us
  waiting for transfers between devices: 69.1 us -> 0.01 us
  other arithmetic: 14.1 us -> 0 us
  starting transfers between devices: 10.3 us -> 0.68 us
    pallas_call x0 -> x4, Pallas kernels: none -> 105 us  [the longest x3 100 us: _grad(): pl.pallas_call(_grad_kernel, grid=(cnt, nb), out_shape=jax.ShapeDtypeStru...]
    dot_general x2 -> x0, matrix products: 97.3 us -> none  [the longest x1 48.7 us: body(): d1 = lax.dot_general(h, dz, tn, preferred_element_type=F32)]
    ppermute x3 -> x2, waiting for transfers between devices: 69.1 us -> 0.01 us  [the longest x1 0.01 us: body(): far = lax.ppermute(mine, 'stage', [(q, (q + S // 2) % S) for q in range(S)])]
    select_n x1 -> x0, other arithmetic: 14.1 us -> none  [body(): jnp.where(p == 0, r, jnp.where(p == 1, near, jnp.where(p == 2, far, back)))]
    ppermute x3 -> x2, starting transfers between devices: 10.3 us -> 0.68 us  [the longest x1 0.64 us: body(): lax.ppermute(far, 'stage', [(q, q + 1 - 2 * (q % 2)) for q in range(S)])]
  transfers between devices with their start and end apart: 3 -> 2, of which waited for: 1 -> 0; matrix products, arithmetic and copies ran while one was open for 20% -> 0% of each run, Pallas kernels for 0% -> 25%
where the time goes in v2:
time: 400 us; the launch traced here: 399 us
  Pallas kernels  398 us (100%)
    pallas_call x1, Pallas kernels, body(): pl.pallas_call(functools.partial(_pipeline, S, V, M, G), out_shape=[jax.S...  293 us
    pallas_call x3, Pallas kernels, _grad(): pl.pallas_call(_grad_kernel, grid=(cnt, nb), out_shape=jax.ShapeDtypeStru...  100 us
  transfers between devices with their start and end apart: 2, of which 0 were waited for; matrix products, arithmetic and copies ran while one was open for 0% of the time, Pallas kernels for 25%

profile of v2, /device:TPU:9, one launch (start us, length us, event | category | flops | bytes accessed | tf_op | source)
XLA Modules:
  0.0 399.3 jit_solution(6784571355032289312)
XLA Ops:
  0.6 292.6 %pipeline.1 = (bf16[32,256,3072]{2,1,0:T(8,128)(2,1)}, bf16[32,256,3072]{2,1,0:T(8,128)(2,1)}, bf16[32,256,768]{2,1,0:T(8,128)(2,1)}, bf16[32,256,768]{2,1,0:T(8...) custom-call(bf16[16,256,768]{2,1,0:T(8,128)(2,1)} %x.1, bf16[16,256,768]{2,1,0:T(8,128)(2,1)} %g.1, ...), custom_call_target="tpu_custom_call" | custom-call | flops 193273528320 | bytes 100663296 | tf_op jit(solution)/shard_map/pipeline/pallas_call | solution.py:347
  293.2 0.0 collective-permute-start
  293.3 26.1 %grad2.1.rest_0_ = f32[2,3072,768]{2,1,0:T(8,128)} custom-call(bf16[2,4096,3072]{2,1,0:T(8,128)(2,1)} %bitcast.12, bf16[2,4096,768]{2,1,0:T(8,128)(2,1)} %bitcast.15), custom_call_target="tpu_custom_call" | custom-call | flops 19327352832 | bytes 40894464 | tf_op jit(solution)/shard_map/grad2/pallas_call | solution.py:295
  319.3 48.1 %grad1.1 = f32[2,768,3072]{2,1,0:T(8,128)} custom-call(bf16[2,4096,768]{2,1,0:T(8,128)(2,1)} %bitcast.21, bf16[2,4096,3072]{2,1,0:T(8,128)(2,1)} %bitcast.19), custom_call_target="tpu_custom_call" | custom-call | flops 38654705664 | bytes 81788928 | tf_op jit(solution)/shard_map/grad1/pallas_call | solution.py:295
  367.4 0.0 copy-start
  367.4 0.0 copy-start.1
  367.4 0.0 collective-permute-done.far
  367.4 0.6 collective-permute-start.1
  368.0 26.3 %grad3.1 = f32[2,3072,768]{2,1,0:T(8,128)} custom-call(bf16[2,4096,3072]{2,1,0:T(8,128)(2,1)} %bitcast.13, bf16[2,4096,768]{2,1,0:T(8,128)(2,1)} %bitcast.16, f32[2,3072,768]{2,1,0:T(8,128)} %grad2.1.rest_0_), custom_call_target="tpu_custom_call", output_to_operand_aliasing={{}: (2, {})} | custom-call | flops 19327352832 | bytes 40894464 | tf_op jit(solution)/shard_map/grad3/pallas_call | solution.py:295
  394.4 0.0 collective-permute-done.1.back
  394.4 0.0 copy-done
  394.4 0.0 copy-done.1
  394.4 4.7 %assemble.1 = (bf16[16,256,768]{2,1,0:T(8,128)(2,1)}, bf16[16,256,768]{2,1,0:T(8,128)(2,1)}) custom-call(bf16[8,256,768]{2,1,0:T(8,128)(2,1)S(1)} %copy-done, bf16[8,256,768]{2,1,0:T(8,128)(2,1)S(1)} %copy-done.1, bf16[8,256,768]{2,1,0:T(8,128)(2,1)S(1)} %collective-permute-done.far, bf16[8,256,768]{2,1,0:T(8,128)(2,1)S(1)} %collective-permute-done.1.back), custom_call_target="tpu_custom_call" | custom-call | tf_op jit(solution)/shard_map/assemble/pallas_call | solution.py:391
Async XLA Ops:
  293.2 74.2 %collective-permute-start = (bf16[8,256,768]{2,1,0:T(8,128)(2,1)}, bf16[8,256,768]{2,1,0:T(8,128)(2,1)S(1)}, u32[]{:S(2)}, u32[]{:S(2)}) collective-permute-start(bf16[8,256,768]{2,1,0:T(8,128)(2,1)} %get-tuple-element.17.mine), channel_id=1, source_target_pairs={{0,2},{1,3},{2,0},{3,1},{4,6},{5,7},{6,4},{7,5},{8,10},{9,11},{10,... | collective-permute-start | bytes 9437192 | tf_op jit(solution)/shard_map/ppermute | solution.py:383
  367.4 27.0 %copy-start = (bf16[8,256,768]{2,1,0:T(8,128)(2,1)S(1)}, bf16[8,256,768]{2,1,0:T(8,128)(2,1)}, u32[]{:S(2)}) copy-start(bf16[8,256,768]{2,1,0:T(8,128)(2,1)} %get-tuple-element.17.mine) | copy-start | bytes 9437188
  367.4 27.0 %copy-start.1 = (bf16[8,256,768]{2,1,0:T(8,128)(2,1)S(1)}, bf16[8,256,768]{2,1,0:T(8,128)(2,1)}, u32[]{:S(2)}) copy-start(bf16[8,256,768]{2,1,0:T(8,128)(2,1)} %get-tuple-element.18.other) | copy-start | bytes 9437188
  367.4 27.0 %collective-permute-start.1 = (bf16[8,256,768]{2,1,0:T(8,128)(2,1)S(1)}, bf16[8,256,768]{2,1,0:T(8,128)(2,1)S(1)}, u32[]{:S(2)}, u32[]{:S(2)}) collective-permute-start(bf16[8,256,768]{2,1,0:T(8,128)(2,1)S(1)} %collective-permute-done.far), channel_id=1, source_target_pairs={{0,1},{1,0},{2,3},{3,2},{4,5},{5,4},{6,7},{7,6},{8,9},{9,8},{10,11... | collective-permute-start | bytes 9437192 | tf_op jit(solution)/shard_map/ppermute | solution.py:387

commit v3 on v2

--- a/solution.py
+++ b/solution.py
@@ -270,38 +270,137 @@
             0, M, lambda m, c: (pltpu.make_async_copy(fo.at[0], mine.at[0], pair_recv.at[m]).wait(), c)[1], 0)
 
 
-def _grad_kernel(a, b, *rest):
-    rest[-1][0] = lax.dot_general(a[0], b[0], (((0,), (0,)), ((), ())), preferred_element_type=F32)
-
-
-def _grad(name, a, b, wide, layers, into=None):
-    V, T, A = a.shape
-    N = b.shape[-1]
-    lo, cnt = layers
-    block = 512 if max(A, N) % 512 == 0 else max(A, N)
-    nb = (A if wide == 0 else N) // block
-    if wide == 0:
-        specs = [pl.BlockSpec((1, T, block), lambda v, i: (v + lo, 0, i)), pl.BlockSpec((1, T, N), lambda v, i: (v + lo, 0, 0))]
-        out = pl.BlockSpec((1, block, N), lambda v, i: (v + lo, i, 0))
-    else:
-        specs = [pl.BlockSpec((1, T, A), lambda v, i: (v + lo, 0, 0)), pl.BlockSpec((1, T, block), lambda v, i: (v + lo, 0, i))]
-        out = pl.BlockSpec((1, A, block), lambda v, i: (v + lo, 0, i))
-    args = [a, b]
-    alias = {}
-    if into is not None:
-        args.append(into)
-        specs.append(pl.BlockSpec(memory_space=pl.ANY))
-        alias = {2: 0}
+def _grads(phases, block, pieces, h, dz, u, dy, *rest):
+    d1, d2, narrow, wide, o1, o2, n_sem, w_sem, o_sem, p_sem = rest[-10:]
+    T, N = wide.shape[1:]
+    nb = dz.shape[-1] // block
+    total = len(phases) * nb
+    tn = (((0,), (0,)), ((), ()))
+
+    def pick(s, values):
+        out = jnp.int32(values[0])
+        for q in range(1, len(values)):
+            out = jnp.where(s // nb == q, values[q], out)
+        return out
+
+    kinds = [k for k, _ in phases]
+    layers = [v for _, v in phases]
+
+    def narrow_copy(q, act):
+        kind, v = phases[q]
+        src = dy if kind else h
+        act(pltpu.make_async_copy(src.at[v], narrow.at[q % 2], n_sem.at[q % 2]))
+
+    def wide_copy(s, act):
+        kind, v = pick(s, kinds), pick(s, layers)
+        slot = lax.rem(s, 2)
+        cols = pl.ds(pl.multiple_of(lax.rem(s, nb) * block, block), block)
+        for k, src in ((0, dz), (1, u)):
+            if k in kinds:
+                @pl.when(kind == k)
+                def _():
+                    act(pltpu.make_async_copy(src.at[v, :, cols], wide.at[slot], w_sem.at[slot]))
+
+    def out_copy(s, act):
+        kind, v = pick(s, kinds), pick(s, layers)
+        slot = lax.rem(s, 2)
+        cols = pl.ds(pl.multiple_of(lax.rem(s, nb) * block, block), block)
+        if 0 in kinds:
+            @pl.when(kind == 0)
+            def _():
+                act(pltpu.make_async_copy(o1.at[slot], d1.at[v, :, cols], o_sem.at[slot]))
+        if 1 in kinds:
+            @pl.when(kind == 1)
+            def _():
+                act(pltpu.make_async_copy(o2.at[slot], d2.at[v, cols, :], o_sem.at[slot]))
+
+    start = lambda c: c.start()
+    wait = lambda c: c.wait()
+
+    kind0, v0 = phases[0]
+    rows = T // pieces
+
+    def piece(r, act):
+        sl = pl.ds(r * rows, rows)
+        act(pltpu.make_async_copy((dy if kind0 else h).at[v0, sl], narrow.at[0, sl], p_sem.at[2 * r]))
+        act(pltpu.make_async_copy((u if kind0 else dz).at[v0, sl, pl.ds(0, block)], wide.at[0, sl], p_sem.at[2 * r + 1]))
+
+    for r in range(pieces):
+        piece(r, start)
+    wide_copy(jnp.int32(1), start)
+    if len(phases) > 1:
+        narrow_copy(1, start)
+
+    for r in range(pieces):
+        piece(r, wait)
+        sl = slice(r * rows, (r + 1) * rows)
+        if kind0:
+            part = lax.dot_general(wide[0, sl], narrow[0, sl], tn, preferred_element_type=F32)
+            o2[0] = part if r == 0 else o2[0] + part
+        else:
+            part = lax.dot_general(narrow[0, sl], wide[0, sl], tn, preferred_element_type=F32)
+            o1[0] = part if r == 0 else o1[0] + part
+    out_copy(jnp.int32(0), start)
+
+    def step(s, carry):
+        slot = lax.rem(s, 2)
+        kind = pick(s, kinds)
+        side = lax.rem(s // nb, 2)
+        wide_copy(s, wait)
+        for q in range(1, len(phases)):
+            @pl.when(s == q * nb)
+            def _():
+                narrow_copy(q, wait)
+                if q + 1 < len(phases):
+                    narrow_copy(q + 1, start)
+
+        @pl.when(s + 1 < total)
+        def _():
+            wide_copy(s + 1, start)
+
+        @pl.when(s >= 2)
+        def _():
+            out_copy(s - 2, wait)
+
+        if 0 in kinds:
+            @pl.when(kind == 0)
+            def _():
+                o1[slot] = lax.dot_general(narrow[side], wide[slot], tn, preferred_element_type=F32)
+        if 1 in kinds:
+            @pl.when(kind == 1)
+            def _():
+                o2[slot] = lax.dot_general(wide[slot], narrow[side], tn, preferred_element_type=F32)
+        out_copy(s, start)
+        return carry
+
+    lax.fori_loop(1, total, step, jnp.int32(0))
+    for s in (total - 2, total - 1):
+        out_copy(jnp.int32(s), wait)
+
+
+def _grad(name, phases, h, dz, u, dy, into=None):
+    V, T, D = h.shape
+    F = dz.shape[-1]
+    block = 1024 if F % 1024 == 0 else F // 2
+    dma = pltpu.SemaphoreType.DMA
+    pieces = 4
+    args = [h, dz, u, dy] + list(into or ())
     return pl.pallas_call(
-        _grad_kernel,
-        grid=(cnt, nb),
-        out_shape=jax.ShapeDtypeStruct((V, A, N), F32),
-        in_specs=specs,
-        out_specs=out,
-        input_output_aliases=alias,
-        compiler_params=pltpu.CompilerParams(vmem_limit_bytes=48 * 2 ** 20),
+        functools.partial(_grads, phases, block, pieces),
+        out_shape=[jax.ShapeDtypeStruct((V, D, F), F32), jax.ShapeDtypeStruct((V, F, D), F32)],
+        in_specs=[pl.BlockSpec(memory_space=pl.ANY)] * len(args),
+        out_specs=[pl.BlockSpec(memory_space=pl.ANY)] * 2,
+        scratch_shapes=[
+            pltpu.VMEM((2, T, D), BF),
+            pltpu.VMEM((2, T, block), BF),
+            pltpu.VMEM((2, D, block), F32),
+            pltpu.VMEM((2, block, D), F32),
+            dma((2,)), dma((2,)), dma((2,)), dma((2 * pieces,)),
+        ],
+        input_output_aliases={4: 0, 5: 1} if into else {},
+        compiler_params=pltpu.CompilerParams(vmem_limit_bytes=54 * 2 ** 20),
         cost_estimate=pl.CostEstimate(
-            flops=2 * cnt * T * A * N, bytes_accessed=cnt * (2 * T * (A + N) + 4 * A * N), transcendentals=0),
+            flops=2 * len(phases) * T * D * F, bytes_accessed=len(phases) * (2 * T * (D + F) + 4 * D * F), transcendentals=0),
         name=name,
     )(*args)
 
@@ -381,12 +480,12 @@
         dy = dy.reshape(V, M * B, D)
 
         far = lax.ppermute(mine, 'stage', [(q, (q + S // 2) % S) for q in range(S)])
-        d1 = _grad('grad1', h, dz, 1, (0, V))
-        d2 = _grad('grad2', u, dy, 0, (0, V - 1))
+        todo = [(0, v) for v in range(V)] + [(1, v) for v in range(V)]
+        d1, d2 = _grad('grads', todo[:-1], h, dz, u, dy)
         far, d1, d2 = lax.optimization_barrier((far, d1, d2))
         back = lax.ppermute(far, 'stage', [(q, q + 1 - 2 * (q % 2)) for q in range(S)])
-        d2 = _grad('grad3', u, dy, 0, (V - 1, 1), d2)
-        back, d2 = lax.optimization_barrier((back, d2))
+        d1, d2 = _grad('grads_last', todo[-1:], h, dz, u, dy, (d1, d2))
+        back, d1, d2 = lax.optimization_barrier((back, d1, d2))
         full = jax.ShapeDtypeStruct((M, B, D), BF)
         y, dx = pl.pallas_call(
             functools.partial(_assemble, S, M),

time: 400 us -> 400 us (level)
  Pallas kernels: 398 us -> 394 us
    pallas_call x3 -> x2, Pallas kernels: 100 us -> 94.4 us  [_grad(): pl.pallas_call(functools.partial(_grads, phases, block, pieces), out_shap...]
  transfers between devices with their start and end apart: 2 -> 2, of which waited for: 0 -> 1; matrix products, arithmetic and copies ran while one was open for 0% -> 0% of each run, Pallas kernels for 25% -> 24%
where the time goes in v3:
time: 400 us
  Pallas kernels  394 us (98%)
    pallas_call x1, Pallas kernels, body(): pl.pallas_call(functools.partial(_pipeline, S, V, M, G), out_shape=[jax.S...  293 us
    pallas_call x2, Pallas kernels, _grad(): pl.pallas_call(functools.partial(_grads, phases, block, pieces), out_shap...  94.4 us
  transfers between devices with their start and end apart: 2, of which 1 were waited for; matrix products, arithmetic and copies ran while one was open for 0% of the time, Pallas kernels for 24%

profile of v3, /device:TPU:9, one launch (start us, length us, event | category | flops | bytes accessed | tf_op | source)
XLA Modules:
  0.0 399.5 jit_solution(2525318895502687622)
XLA Ops:
  0.6 292.6 %pipeline.1 = (bf16[32,256,3072]{2,1,0:T(8,128)(2,1)}, bf16[32,256,3072]{2,1,0:T(8,128)(2,1)}, bf16[32,256,768]{2,1,0:T(8,128)(2,1)}, bf16[32,256,768]{2,1,0:T(8...) custom-call(bf16[16,256,768]{2,1,0:T(8,128)(2,1)} %x.1, bf16[16,256,768]{2,1,0:T(8,128)(2,1)} %g.1, ...), custom_call_target="tpu_custom_call" | custom-call | flops 193273528320 | bytes 100663296 | tf_op jit(solution)/shard_map/pipeline/pallas_call | solution.py:446
  293.2 0.0 collective-permute-start
  293.3 65.5 %grads.1 = (f32[2,768,3072]{2,1,0:T(8,128)}, f32[2,3072,768]{2,1,0:T(8,128)}) custom-call(bf16[2,4096,768]{2,1,0:T(8,128)(2,1)} %bitcast.18, bf16[2,4096,3072]{2,1,0:T(8,128)(2,1)} %bitcast.14, bf16[2,4096,3072]{2,1,0:T(8,128)(2,1)} %bitcast.12, bf16[2,4096,768]{2,1,0:T(8,128)(2,1)} %bitcast.20), custom_call_target="tpu_custom_call" | custom-call | flops 57982058496 | bytes 122683392 | tf_op jit(solution)/shard_map/grads/pallas_call | solution.py:388
  358.8 3.7 collective-permute-done.far
  362.5 0.0 copy-start
  362.5 0.0 copy-start.1
  362.5 1.3 collective-permute-start.1
  363.8 28.9 %grads_last.1 = (f32[2,768,3072]{2,1,0:T(8,128)}, f32[2,3072,768]{2,1,0:T(8,128)}) custom-call(bf16[2,4096,768]{2,1,0:T(8,128)(2,1)} %bitcast.19, bf16[2,4096,3072]{2,1,0:T(8,128)(2,1)} %bitcast.15, bf16[2,4096,3072]{2,1,0:T(8,128)(2,1)} %bitcast.13, bf16[2,4096,768]{2,1,0:T(8,128)(2,1)} %bitcast.21, ...), custom_call_target="tpu_custom_call", output_to_operand_aliasing={{0}: (4, {}), {1}: (5, {})} | custom-call | flops 19327352832 | bytes 40894464 | tf_op jit(solution)/shard_map/grads_last/pallas_call | solution.py:388
  392.7 0.0 collective-permute-done.1.back
  392.7 0.0 copy-done
  392.7 0.0 copy-done.1
  392.7 6.6 %assemble.1 = (bf16[16,256,768]{2,1,0:T(8,128)(2,1)}, bf16[16,256,768]{2,1,0:T(8,128)(2,1)}) custom-call(bf16[8,256,768]{2,1,0:T(8,128)(2,1)S(1)} %copy-done, bf16[8,256,768]{2,1,0:T(8,128)(2,1)S(1)} %copy-done.1, bf16[8,256,768]{2,1,0:T(8,128)(2,1)S(1)} %collective-permute-done.far, bf16[8,256,768]{2,1,0:T(8,128)(2,1)} %collective-permute-done.1.back), custom_call_target="tpu_custom_call" | custom-call | tf_op jit(solution)/shard_map/assemble/pallas_call | solution.py:490
Async XLA Ops:
  293.2 69.3 %collective-permute-start = (bf16[8,256,768]{2,1,0:T(8,128)(2,1)}, bf16[8,256,768]{2,1,0:T(8,128)(2,1)S(1)}, u32[]{:S(2)}, u32[]{:S(2)}) collective-permute-start(bf16[8,256,768]{2,1,0:T(8,128)(2,1)} %get-tuple-element.22.mine), channel_id=1, source_target_pairs={{0,2},{1,3},{2,0},{3,1},{4,6},{5,7},{6,4},{7,5},{8,10},{9,11},{10,... | collective-permute-start | bytes 9437192 | tf_op jit(solution)/shard_map/ppermute | solution.py:482
  362.5 30.2 %copy-start = (bf16[8,256,768]{2,1,0:T(8,128)(2,1)S(1)}, bf16[8,256,768]{2,1,0:T(8,128)(2,1)}, u32[]{:S(2)}) copy-start(bf16[8,256,768]{2,1,0:T(8,128)(2,1)} %get-tuple-element.22.mine) | copy-start | bytes 9437188
  362.5 30.2 %copy-start.1 = (bf16[8,256,768]{2,1,0:T(8,128)(2,1)S(1)}, bf16[8,256,768]{2,1,0:T(8,128)(2,1)}, u32[]{:S(2)}) copy-start(bf16[8,256,768]{2,1,0:T(8,128)(2,1)} %get-tuple-element.23.other) | copy-start | bytes 9437188
  362.5 30.2 %collective-permute-start.1 = (bf16[8,256,768]{2,1,0:T(8,128)(2,1)S(1)}, bf16[8,256,768]{2,1,0:T(8,128)(2,1)}, u32[]{:S(2)}, u32[]{:S(2)}) collective-permute-start(bf16[8,256,768]{2,1,0:T(8,128)(2,1)S(1)} %collective-permute-done.far), channel_id=1, source_target_pairs={{0,1},{1,0},{2,3},{3,2},{4,5},{5,4},{6,7},{7,6},{8,9},{9,8},{10,11... | collective-permute-start | bytes 9437192 | tf_op jit(solution)/shard_map/ppermute | solution.py:486

commit v4 on v3

--- a/solution.py
+++ b/solution.py
@@ -13,12 +13,12 @@
 NT = (((1,), (1,)), ((), ()))
 GROUP = 8
 ORDER = (
-    'FFFFFFFFFFFFFFFFFFFFFFFBFBBBBFBFBFBFBFBFBFBFBBBBBBBBBBBBBBBBBBBB',
-    'FFFFFFFFFFFFFFFFFFFBFBFBFBFBFBBFBFBFBFBFBFBFBFBBBBBBBBBBBBBBBBBB',
-    'FFFFFFFFFFFBFFBFBFBFBFBFBFBFBFBFBFBFBFBFBFBFBFBFBFBFBBBBBBBBBBBB',
-    'FFFFFFFFBBBFBBFBFBFBBFFFBFBFBFBFBFBFBBFBFBFBFBFBFBFBBBBBFBBBBFFF',
+    'FFFFFFFFFFFFFFFFFFFFFBFBFBBBFMMMBFFMMBMBBBBBBBBBBBBBBBBBBB',
+    'FFFFFFFFFFFFFFFFFMFBFMBBFBFMBMFBFMFBFBFBMBBBBBBBBBBBBBBBBB',
+    'FFFFFFFFFFFMFMBMMMMMMMMMMMMMMFBMMMBBBBBBBBBBB',
+    'FFFFFFFFBBBBFFBBFBMMMMMMMMMMMMMMMMMBBBMBBBBFFF',
 )
-WORD = 16
+WORD = 15
 
 
 def _gelu(z):
@@ -39,7 +39,7 @@
 
 
 def _words(row):
-    return [sum((c == 'B') << b for b, c in enumerate(row[k:k + WORD])) for k in range(0, len(row), WORD)]
+    return [sum('FBM'.index(c) * 4 ** b for b, c in enumerate(row[k:k + WORD])) for k in range(0, len(row), WORD)]
 
 
 def _pipeline(S, V, M, G, x, g, w1_hbm, w2_hbm, u_out, dz_out, h_out, dy_out, mine, other,
@@ -131,78 +131,79 @@
         pltpu.make_async_copy(fo.at[0], hbuf.at[slot], f_recv.at[slot]).wait()
         pltpu.make_async_copy(hbuf.at[slot], h_out.at[slot], h_sem.at[slot]).start()
 
-    def finish(src, s, m, sem):
-        k = lax.rem(m, H)
-        upper = m // H
-        own = upper == parity
-
-        def send(here, there):
-            pltpu.make_async_copy(src.at[s], here.at[k], sem.at[s]).start()
-            pltpu.make_async_remote_copy(
-                src_ref=src.at[s], dst_ref=there.at[k], send_sem=pair_send.at[s], recv_sem=pair_recv.at[m],
-                device_id={'stage': partner}, device_id_type=MESH).start()
+    def halves(m, put):
+        own = m // H == parity
 
         @pl.when(own)
         def _():
-            send(mine, other)
+            put(mine, other)
 
         @pl.when(jnp.logical_not(own))
         def _():
-            send(other, mine)
-
-    def forward(i):
+            put(other, mine)
+
+    def ready_f(i):
+        v, m = place_f(i)
+
+        @pl.when(i == G - 1)
+        def _():
+            for vv in range(1, V):
+                wait_w(vv)
+
+        @pl.when(jnp.logical_not(last & (v == V - 1)))
+        def _():
+            take_h(v * M + m)
+
+        @pl.when(i >= 2)
+        def _():
+            wait_f_send(i - 2)
+
+    def compute_f(i):
         v, m = place_f(i)
         slot = v * M + m
         s = lax.rem(i, 2)
-        final = last & (v == V - 1)
-
-        @pl.when(i == G - 1)
-        def _():
-            for vv in range(1, V):
-                wait_w(vv)
-
-        @pl.when(jnp.logical_not(final))
-        def _():
-            take_h(slot)
-
-        @pl.when(i >= 2)
-        def _():
-            wait_f_send(i - 2)
-
         for c in range(F // chunk):
             cs = slice(c * chunk, (c + 1) * chunk)
             us[:, cs] = _gelu(_dot(hbuf[slot], w1[v, :, cs])).astype(BF)
         fo[s] = (hbuf[slot].astype(F32) + _dot(us[...], w2[v])).astype(BF)
-
-        @pl.when(final)
-        def _():
-            finish(fo, s, m, f_send)
-
-        @pl.when(jnp.logical_not(final))
-        def _():
-            to = slot + jnp.where(last, M, 0)
-            pltpu.make_async_remote_copy(
-                src_ref=fo.at[s], dst_ref=hbuf.at[to], send_sem=f_send.at[s], recv_sem=f_recv.at[to],
-                device_id={'stage': nxt}, device_id_type=MESH).start()
-
-    def backward(j):
+        to = slot + jnp.where(last, M, 0)
+        pltpu.make_async_remote_copy(
+            src_ref=fo.at[s], dst_ref=hbuf.at[to], send_sem=f_send.at[s], recv_sem=f_recv.at[to],
+            device_id={'stage': jnp.where(last & (v == V - 1), partner, nxt)}, device_id_type=MESH).start()
+
+    def done_f(i):
+        v, m = place_f(i)
+        s = lax.rem(i, 2)
+
+        @pl.when(last & (v == V - 1))
+        def _():
+            halves(m, lambda here, there: pltpu.make_async_copy(
+                fo.at[s], here.at[lax.rem(m, H)], pair_send.at[s]).start())
+
+    def place_b(j):
         vr, m = place(j)
-        v = V - 1 - vr
+        return V - 1 - vr, m
+
+    def ready_b(j):
+        v, m = place_b(j)
+        slot = v * M + m
+
+        @pl.when(last & (v == V - 1))
+        def _():
+            take_h(slot)
+
+        pltpu.make_async_copy(bo.at[0], dybuf.at[slot], b_recv.at[slot]).wait()
+        pltpu.make_async_copy(dybuf.at[slot], dy_out.at[slot], dy_sem.at[slot]).start()
+
+        @pl.when(j >= 2)
+        def _():
+            wait_b_send(j - 2)
+            wait_uz(lax.rem(j, 2))
+
+    def compute_b(j):
+        v, m = place_b(j)
         slot = v * M + m
         s = lax.rem(j, 2)
-
-        @pl.when(last & (v == V - 1))
-        def _():
-            take_h(slot)
-
-        pltpu.make_async_copy(bo.at[0], dybuf.at[slot], b_recv.at[slot]).wait()
-        pltpu.make_async_copy(dybuf.at[slot], dy_out.at[slot], dy_sem.at[slot]).start()
-
-        @pl.when(j >= 2)
-        def _():
-            wait_b_send(j - 2)
-            wait_uz(s)
-
         for c in range(F // chunk):
             cs = slice(c * chunk, (c + 1) * chunk)
             a, b = _gelu_pair(_dot(hbuf[slot], w1[v, :, cs]))
@@ -212,11 +213,23 @@
         bo[s] = (dybuf[slot].astype(F32) + _dot_nt(dzb[s], w1[v])).astype(BF)
         pltpu.make_async_copy(dzb.at[s], dz_out.at[slot], dz_sem.at[s]).start()
 
+    def done_b(j):
+        v, m = place_b(j)
+        slot = v * M + m
+        s = lax.rem(j, 2)
         final = first & (v == 0)
 
         @pl.when(final)
         def _():
-            finish(bo, s, m, b_send)
+            k = lax.rem(m, H)
+
+            def put(here, there):
+                pltpu.make_async_copy(bo.at[s], here.at[k], b_send.at[s]).start()
+                pltpu.make_async_remote_copy(
+                    src_ref=bo.at[s], dst_ref=there.at[k], send_sem=pair_send.at[s], recv_sem=pair_recv.at[m],
+                    device_id={'stage': partner}, device_id_type=MESH).start()
+
+            halves(m, put)
 
         @pl.when(jnp.logical_not(final))
         def _():
@@ -230,33 +243,62 @@
     def word(k):
         out = jnp.int32(0)
         for q in range(S):
-            for b in range(2 * n // WORD):
+            for b in range(len(table[q])):
                 out = jnp.where((p == q) & (k == b), table[q][b], out)
         return out
 
     def step(t, carry):
         i, j, bits = carry
         bits = jnp.where(lax.rem(t, WORD) == 0, word(t // WORD), bits)
-        back = lax.rem(bits, 2)
-
-        @pl.when(back == 0)
-        def _():
-            forward(i)
-
-        @pl.when(back == 1)
-        def _():
-            backward(j)
-
-        return i + 1 - back, j + back, bits // 2
+        kind = lax.rem(bits, 4)
+
+        @pl.when(kind == 0)
+        def _():
+            ready_f(i)
+            compute_f(i)
+            done_f(i)
+
+        @pl.when(kind == 1)
+        def _():
+            ready_b(j)
+            compute_b(j)
+            done_b(j)
+
+        @pl.when(kind == 2)
+        def _():
+            ready_f(i)
+            ready_b(j)
+            compute_f(i)
+            compute_b(j)
+            done_f(i)
+            done_b(j)
+
+        return i + jnp.where(kind == 1, 0, 1), j + jnp.where(kind == 0, 0, 1), bits // 4
 
     zero = jnp.int32(0)
-    lax.fori_loop(0, 2 * n, step, (zero, zero, zero))
+    count = jnp.int32(0)
+    for q in range(S):
+        count = jnp.where(p == q, len(ORDER[q]), count)
+    lax.fori_loop(0, count, step, (zero, zero, zero))
 
     for k in (n - 2, n - 1):
         wait_f_send(jnp.int32(k))
         wait_b_send(jnp.int32(k))
         wait_uz(k % 2)
 
+    @pl.when(p == S - 2)
+    def _():
+        def take(m, c):
+            pltpu.make_async_copy(fo.at[0], hbuf.at[n + m], f_recv.at[n + m]).wait()
+            return c
+
+        lax.fori_loop(0, M, take, 0)
+        copies = [pltpu.make_async_copy(hbuf.at[pl.ds(n + k * H, H)], ref, pair_send.at[k]) for k, ref in enumerate((mine, other))]
+        for c in copies:
+            c.start()
+        for c in copies:
+            c.wait()
+
     def drain(slot, carry):
         pltpu.make_async_copy(hbuf.at[slot], h_out.at[slot], h_sem.at[slot]).wait()
         pltpu.make_async_copy(dybuf.at[slot], dy_out.at[slot], dy_sem.at[slot]).wait()
@@ -264,37 +306,36 @@
 
     lax.fori_loop(0, n, drain, 0)
 
-    @pl.when(jnp.logical_not(first | last))
+    @pl.when(p == 1)
     def _():
         lax.fori_loop(
             0, M, lambda m, c: (pltpu.make_async_copy(fo.at[0], mine.at[0], pair_recv.at[m]).wait(), c)[1], 0)
 
 
-def _grads(phases, block, pieces, h, dz, u, dy, *rest):
+def _grads(work, block, pieces, h, dz, u, dy, *rest):
     d1, d2, narrow, wide, o1, o2, n_sem, w_sem, o_sem, p_sem = rest[-10:]
-    T, N = wide.shape[1:]
-    nb = dz.shape[-1] // block
-    total = len(phases) * nb
+    T = wide.shape[1]
+    begin = [sum(w[3] for w in work[:q]) for q in range(len(work) + 1)]
+    total = begin[-1]
     tn = (((0,), (0,)), ((), ()))
+    kinds = [w[0] for w in work]
 
     def pick(s, values):
         out = jnp.int32(values[0])
-        for q in range(1, len(values)):
-            out = jnp.where(s // nb == q, values[q], out)
+        for q in range(1, len(work)):
+            out = jnp.where(s >= begin[q], values[q], out)
         return out
 
-    kinds = [k for k, _ in phases]
-    layers = [v for _, v in phases]
+    def at(s):
+        v = pick(s, [w[1] for w in work])
+        blk = s + pick(s, [w[2] - begin[q] for q, w in enumerate(work)])
+        return pick(s, kinds), v, pl.ds(pl.multiple_of(blk * block, block), block), lax.rem(s, 2)
 
     def narrow_copy(q, act):
-        kind, v = phases[q]
-        src = dy if kind else h
-        act(pltpu.make_async_copy(src.at[v], narrow.at[q % 2], n_sem.at[q % 2]))
+        act(pltpu.make_async_copy((dy if kinds[q] else h).at[work[q][1]], narrow.at[q % 2], n_sem.at[q % 2]))
 
     def wide_copy(s, act):
-        kind, v = pick(s, kinds), pick(s, layers)
-        slot = lax.rem(s, 2)
-        cols = pl.ds(pl.multiple_of(lax.rem(s, nb) * block, block), block)
+        kind, v, cols, slot = at(s)
         for k, src in ((0, dz), (1, u)):
             if k in kinds:
                 @pl.when(kind == k)
@@ -302,9 +343,7 @@
                     act(pltpu.make_async_copy(src.at[v, :, cols], wide.at[slot], w_sem.at[slot]))
 
     def out_copy(s, act):
-        kind, v = pick(s, kinds), pick(s, layers)
-        slot = lax.rem(s, 2)
-        cols = pl.ds(pl.multiple_of(lax.rem(s, nb) * block, block), block)
+        kind, v, cols, slot = at(s)
         if 0 in kinds:
             @pl.when(kind == 0)
             def _():
@@ -316,42 +355,40 @@
 
     start = lambda c: c.start()
     wait = lambda c: c.wait()
-
-    kind0, v0 = phases[0]
     rows = T // pieces
 
     def piece(r, act):
-        sl = pl.ds(r * rows, rows)
-        act(pltpu.make_async_copy((dy if kind0 else h).at[v0, sl], narrow.at[0, sl], p_sem.at[2 * r]))
-        act(pltpu.make_async_copy((u if kind0 else dz).at[v0, sl, pl.ds(0, block)], wide.at[0, sl], p_sem.at[2 * r + 1]))
+        sl = pl.ds(pl.multiple_of(r * rows, rows), rows)
+        act(pltpu.make_async_copy(h.at[work[0][1], sl], narrow.at[0, sl], p_sem.at[2 * r]))
+        act(pltpu.make_async_copy(dz.at[work[0][1], sl, pl.ds(work[0][2] * block, block)], wide.at[0, sl], p_sem.at[2 * r + 1]))
 
     for r in range(pieces):
         piece(r, start)
     wide_copy(jnp.int32(1), start)
-    if len(phases) > 1:
+    if len(work) > 1:
         narrow_copy(1, start)
 
-    for r in range(pieces):
+    piece(0, wait)
+    o1[0] = lax.dot_general(narrow[0, :rows], wide[0, :rows], tn, preferred_element_type=F32)
+
+    def add(r, carry):
         piece(r, wait)
-        sl = slice(r * rows, (r + 1) * rows)
-        if kind0:
-            part = lax.dot_general(wide[0, sl], narrow[0, sl], tn, preferred_element_type=F32)
-            o2[0] = part if r == 0 else o2[0] + part
-        else:
-            part = lax.dot_general(narrow[0, sl], wide[0, sl], tn, preferred_element_type=F32)
-            o1[0] = part if r == 0 else o1[0] + part
+        sl = pl.ds(pl.multiple_of(r * rows, rows), rows)
+        o1[0] += lax.dot_general(narrow[0, sl], wide[0, sl], tn, preferred_element_type=F32)
+        return carry
+
+    lax.fori_loop(1, pieces, add, jnp.int32(0))
     out_copy(jnp.int32(0), start)
 
     def step(s, carry):
-        slot = lax.rem(s, 2)
-        kind = pick(s, kinds)
-        side = lax.rem(s // nb, 2)
+        kind, _, _, slot = at(s)
+        side = pick(s, [q % 2 for q in range(len(work))])
         wide_copy(s, wait)
-        for q in range(1, len(phases)):
-            @pl.when(s == q * nb)
+        for q in range(1, len(work)):
+            @pl.when(s == begin[q])
             def _():
                 narrow_copy(q, wait)
-                if q + 1 < len(phases):
+                if q + 1 < len(work):
                     narrow_copy(q + 1, start)
 
         @pl.when(s + 1 < total)
@@ -378,15 +415,14 @@
         out_copy(jnp.int32(s), wait)
 
 
-def _grad(name, phases, h, dz, u, dy, into=None):
+def _grad(name, work, block, h, dz, u, dy, into=None):
     V, T, D = h.shape
     F = dz.shape[-1]
-    block = 1024 if F % 1024 == 0 else F // 2
     dma = pltpu.SemaphoreType.DMA
     pieces = 4
     args = [h, dz, u, dy] + list(into or ())
     return pl.pallas_call(
-        functools.partial(_grads, phases, block, pieces),
+        functools.partial(_grads, work, block, pieces),
         out_shape=[jax.ShapeDtypeStruct((V, D, F), F32), jax.ShapeDtypeStruct((V, F, D), F32)],
         in_specs=[pl.BlockSpec(memory_space=pl.ANY)] * len(args),
         out_specs=[pl.BlockSpec(memory_space=pl.ANY)] * 2,
@@ -400,7 +436,7 @@
         input_output_aliases={4: 0, 5: 1} if into else {},
         compiler_params=pltpu.CompilerParams(vmem_limit_bytes=54 * 2 ** 20),
         cost_estimate=pl.CostEstimate(
-            flops=2 * len(phases) * T * D * F, bytes_accessed=len(phases) * (2 * T * (D + F) + 4 * D * F), transcendentals=0),
+            flops=2 * sum(w[3] for w in work) * T * D * block, bytes_accessed=sum(w[3] for w in work) * (2 * T * block + 4 * D * block), transcendentals=0),
         name=name,
     )(*args)
 
@@ -457,14 +493,14 @@
             scratch_shapes=[
                 pltpu.VMEM((V, D, F), BF),
                 pltpu.VMEM((V, F, D), BF),
-                pltpu.VMEM((n, B, D), BF),
+                pltpu.VMEM((n + M, B, D), BF),
                 pltpu.VMEM((n, B, D), BF),
                 pltpu.VMEM((B, F), BF),
                 pltpu.VMEM((2, B, F), BF),
                 pltpu.VMEM((2, B, F), BF),
                 pltpu.VMEM((2, B, D), BF),
                 pltpu.VMEM((2, B, D), BF),
-                dma((n,)), dma((n,)), dma((2,)), dma((2,)),
+                dma((n + M,)), dma((n,)), dma((2,)), dma((2,)),
                 dma((n,)), dma((n,)), dma((2,)), dma((2,)), dma((2 * V,)), dma((2,)), dma((M,)),
             ],
             compiler_params=pltpu.CompilerParams(
@@ -480,11 +516,13 @@
         dy = dy.reshape(V, M * B, D)
 
         far = lax.ppermute(mine, 'stage', [(q, (q + S // 2) % S) for q in range(S)])
-        todo = [(0, v) for v in range(V)] + [(1, v) for v in range(V)]
-        d1, d2 = _grad('grads', todo[:-1], h, dz, u, dy)
+        block = 1024 if F % 1024 == 0 else F // 3 if F % 384 == 0 else F // 2
+        nb = F // block
+        work = [(0, 0, 0, nb)] + [(1, v, 0, nb) for v in range(V)] + [(0, v, 0, nb) for v in range(1, V - 1)]
+        d1, d2 = _grad('grads', work + [(0, V - 1, 0, nb - 2)] * (nb > 2), block, h, dz, u, dy)
         far, d1, d2 = lax.optimization_barrier((far, d1, d2))
         back = lax.ppermute(far, 'stage', [(q, q + 1 - 2 * (q % 2)) for q in range(S)])
-        d1, d2 = _grad('grads_last', todo[-1:], h, dz, u, dy, (d1, d2))
+        d1, d2 = _grad('grads_last', [(0, V - 1, nb - 2, 2)], block, h, dz, u, dy, (d1, d2))
         back, d1, d2 = lax.optimization_barrier((back, d1, d2))
         full = jax.ShapeDtypeStruct((M, B, D), BF)
         y, dx = pl.pallas_call(

time: 400 us -> 394 us (0.985)
  transfers between devices with their start and end apart: 2 -> 2, of which waited for: 1 -> 0; matrix products, arithmetic and copies ran while one was open for 0% -> 0% of each run, Pallas kernels for 24% -> 23%
where the time goes in v4:
time: 394 us; the launch traced here: 393 us
  Pallas kernels  392 us (99%)
    pallas_call x1, Pallas kernels, body(): pl.pallas_call(functools.partial(_pipeline, S, V, M, G), out_shape=[jax.S...  294 us
    pallas_call x2, Pallas kernels, _grad(): pl.pallas_call(functools.partial(_grads, work, block, pieces), out_shape=...  91 us
  transfers between devices with their start and end apart: 2, of which 0 were waited for; matrix products, arithmetic and copies ran while one was open for 0% of the time, Pallas kernels for 23%

profile of v4, /device:TPU:9, one launch (start us, length us, event | category | flops | bytes accessed | tf_op | source)
XLA Modules:
  0.0 393.0 jit_solution(17622888628136383397)
XLA Ops:
  0.6 294.1 %pipeline.1 = (bf16[32,256,3072]{2,1,0:T(8,128)(2,1)}, bf16[32,256,3072]{2,1,0:T(8,128)(2,1)}, bf16[32,256,768]{2,1,0:T(8,128)(2,1)}, bf16[32,256,768]{2,1,0:T(8...) custom-call(bf16[16,256,768]{2,1,0:T(8,128)(2,1)} %x.1, bf16[16,256,768]{2,1,0:T(8,128)(2,1)} %g.1, ...), custom_call_target="tpu_custom_call" | custom-call | flops 193273528320 | bytes 100663296 | tf_op jit(solution)/shard_map/pipeline/pallas_call | solution.py:482
  294.7 0.0 collective-permute-start
  294.8 72.7 %grads.1 = (f32[2,768,3072]{2,1,0:T(8,128)}, f32[2,3072,768]{2,1,0:T(8,128)}) custom-call(bf16[2,4096,768]{2,1,0:T(8,128)(2,1)} %bitcast.18, bf16[2,4096,3072]{2,1,0:T(8,128)(2,1)} %bitcast.14, bf16[2,4096,3072]{2,1,0:T(8,128)(2,1)} %bitcast.12, bf16[2,4096,768]{2,1,0:T(8,128)(2,1)} %bitcast.20), custom_call_target="tpu_custom_call" | custom-call | flops 64424509440 | bytes 115343360 | tf_op jit(solution)/shard_map/grads/pallas_call | solution.py:424
  367.5 0.0 collective-permute-done.far
  367.5 0.0 copy-start
  367.5 0.0 copy-start.1
  367.5 0.5 collective-permute-start.1
  368.0 18.2 %grads_last.1 = (f32[2,768,3072]{2,1,0:T(8,128)}, f32[2,3072,768]{2,1,0:T(8,128)}) custom-call(bf16[2,4096,768]{2,1,0:T(8,128)(2,1)} %bitcast.19, bf16[2,4096,3072]{2,1,0:T(8,128)(2,1)} %bitcast.15, bf16[2,4096,3072]{2,1,0:T(8,128)(2,1)} %bitcast.13, bf16[2,4096,768]{2,1,0:T(8,128)(2,1)} %bitcast.21, ...), custom_call_target="tpu_custom_call", output_to_operand_aliasing={{0}: (4, {}), {1}: (5, {})} | custom-call | flops 12884901888 | bytes 23068672 | tf_op jit(solution)/shard_map/grads_last/pallas_call | solution.py:424
  386.2 0.0 collective-permute-done.1.back
  386.2 0.0 copy-done
  386.2 0.0 copy-done.1
  386.3 6.6 %assemble.1 = (bf16[16,256,768]{2,1,0:T(8,128)(2,1)}, bf16[16,256,768]{2,1,0:T(8,128)(2,1)}) custom-call(bf16[8,256,768]{2,1,0:T(8,128)(2,1)S(1)} %copy-done, bf16[8,256,768]{2,1,0:T(8,128)(2,1)S(1)} %copy-done.1, bf16[8,256,768]{2,1,0:T(8,128)(2,1)S(1)} %collective-permute-done.far, bf16[8,256,768]{2,1,0:T(8,128)(2,1)} %collective-permute-done.1.back), custom_call_target="tpu_custom_call" | custom-call | tf_op jit(solution)/shard_map/assemble/pallas_call | solution.py:528
Async XLA Ops:
  294.7 72.8 %collective-permute-start = (bf16[8,256,768]{2,1,0:T(8,128)(2,1)}, bf16[8,256,768]{2,1,0:T(8,128)(2,1)S(1)}, u32[]{:S(2)}, u32[]{:S(2)}) collective-permute-start(bf16[8,256,768]{2,1,0:T(8,128)(2,1)} %get-tuple-element.22.mine), channel_id=1, source_target_pairs={{0,2},{1,3},{2,0},{3,1},{4,6},{5,7},{6,4},{7,5},{8,10},{9,11},{10,... | collective-permute-start | bytes 9437192 | tf_op jit(solution)/shard_map/ppermute | solution.py:518
  367.5 18.7 %copy-start = (bf16[8,256,768]{2,1,0:T(8,128)(2,1)S(1)}, bf16[8,256,768]{2,1,0:T(8,128)(2,1)}, u32[]{:S(2)}) copy-start(bf16[8,256,768]{2,1,0:T(8,128)(2,1)} %get-tuple-element.22.mine) | copy-start | bytes 9437188
  367.5 18.7 %copy-start.1 = (bf16[8,256,768]{2,1,0:T(8,128)(2,1)S(1)}, bf16[8,256,768]{2,1,0:T(8,128)(2,1)}, u32[]{:S(2)}) copy-start(bf16[8,256,768]{2,1,0:T(8,128)(2,1)} %get-tuple-element.23.other) | copy-start | bytes 9437188
  367.5 18.7 %collective-permute-start.1 = (bf16[8,256,768]{2,1,0:T(8,128)(2,1)S(1)}, bf16[8,256,768]{2,1,0:T(8,128)(2,1)}, u32[]{:S(2)}, u32[]{:S(2)}) collective-permute-start(bf16[8,256,768]{2,1,0:T(8,128)(2,1)S(1)} %collective-permute-done.far), channel_id=1, source_target_pairs={{0,1},{1,0},{2,3},{3,2},{4,5},{5,4},{6,7},{7,6},{8,9},{9,8},{10,11... | collective-permute-start | bytes 9437192 | tf_op jit(solution)/shard_map/ppermute | solution.py:524

commit v5 on v4

--- a/solution.py
+++ b/solution.py
@@ -13,10 +13,10 @@
 NT = (((1,), (1,)), ((), ()))
 GROUP = 8
 ORDER = (
-    'FFFFFFFFFFFFFFFFFFFFFBFBFBBBFMMMBFFMMBMBBBBBBBBBBBBBBBBBBB',
-    'FFFFFFFFFFFFFFFFFMFBFMBBFBFMBMFBFMFBFBFBMBBBBBBBBBBBBBBBBB',
-    'FFFFFFFFFFFMFMBMMMMMMMMMMMMMMFBMMMBBBBBBBBBBB',
-    'FFFFFFFFBBBBFFBBFBMMMMMMMMMMMMMMMMMBBBMBBBBFFF',
+    'FFFFFFFFFFFFFFFFFFFFFBFMBBFBFBFBFBBFBFFBFBFBBBBBBBBBBBBBBBBBBBB',
+    'FFFFFFFFFFFFFFFFFFBFFMBBBFBFBFBFBMFBFMFBFMBBBBBBBBBBBBBBBBBB',
+    'FFFFFFFFFFFBFMFMMMMMMMMMMMBMMMMMMMBBBBBBBBBBB',
+    'FFFFFFFFBFBMBBBMBFFBFBMBMFMMFFMMMMMBMMBBBBBBBBBFFFF',
 )
 WORD = 15
 
@@ -166,19 +166,31 @@
             cs = slice(c * chunk, (c + 1) * chunk)
             us[:, cs] = _gelu(_dot(hbuf[slot], w1[v, :, cs])).astype(BF)
         fo[s] = (hbuf[slot].astype(F32) + _dot(us[...], w2[v])).astype(BF)
-        to = slot + jnp.where(last, M, 0)
-        pltpu.make_async_remote_copy(
-            src_ref=fo.at[s], dst_ref=hbuf.at[to], send_sem=f_send.at[s], recv_sem=f_recv.at[to],
-            device_id={'stage': jnp.where(last & (v == V - 1), partner, nxt)}, device_id_type=MESH).start()
 
     def done_f(i):
         v, m = place_f(i)
+        slot = v * M + m
         s = lax.rem(i, 2)
-
-        @pl.when(last & (v == V - 1))
-        def _():
-            halves(m, lambda here, there: pltpu.make_async_copy(
-                fo.at[s], here.at[lax.rem(m, H)], pair_send.at[s]).start())
+        final = last & (v == V - 1)
+
+        @pl.when(final)
+        def _():
+            k = lax.rem(m, H)
+
+            def put(here, there):
+                pltpu.make_async_copy(fo.at[s], here.at[k], f_send.at[s]).start()
+                pltpu.make_async_remote_copy(
+                    src_ref=fo.at[s], dst_ref=there.at[k], send_sem=pair_send.at[s], recv_sem=pair_recv.at[m],
+                    device_id={'stage': partner}, device_id_type=MESH).start()
+
+            halves(m, put)
+
+        @pl.when(jnp.logical_not(final))
+        def _():
+            to = slot + jnp.where(last, M, 0)
+            pltpu.make_async_remote_copy(
+                src_ref=fo.at[s], dst_ref=hbuf.at[to], send_sem=f_send.at[s], recv_sem=f_recv.at[to],
+                device_id={'stage': nxt}, device_id_type=MESH).start()
 
     def place_b(j):
         vr, m = place(j)
@@ -211,32 +223,22 @@
             dzb[s, :, cs] = (_dot_nt(dybuf[slot], w2[v, cs, :]) * b).astype(BF)
         pltpu.make_async_copy(ub.at[s], u_out.at[slot], u_sem.at[s]).start()
         bo[s] = (dybuf[slot].astype(F32) + _dot_nt(dzb[s], w1[v])).astype(BF)
-        pltpu.make_async_copy(dzb.at[s], dz_out.at[slot], dz_sem.at[s]).start()
 
     def done_b(j):
         v, m = place_b(j)
         slot = v * M + m
         s = lax.rem(j, 2)
         final = first & (v == 0)
+        to = jnp.where(final, n + m, slot - jnp.where(first, M, 0))
+        pltpu.make_async_remote_copy(
+            src_ref=bo.at[s], dst_ref=dybuf.at[to], send_sem=b_send.at[s], recv_sem=b_recv.at[to],
+            device_id={'stage': jnp.where(final, partner, prv)}, device_id_type=MESH).start()
+        pltpu.make_async_copy(dzb.at[s], dz_out.at[slot], dz_sem.at[s]).start()
 
         @pl.when(final)
         def _():
-            k = lax.rem(m, H)
-
-            def put(here, there):
-                pltpu.make_async_copy(bo.at[s], here.at[k], b_send.at[s]).start()
-                pltpu.make_async_remote_copy(
-                    src_ref=bo.at[s], dst_ref=there.at[k], send_sem=pair_send.at[s], recv_sem=pair_recv.at[m],
-                    device_id={'stage': partner}, device_id_type=MESH).start()
-
-            halves(m, put)
-
-        @pl.when(jnp.logical_not(final))
-        def _():
-            to = slot - jnp.where(first, M, 0)
-            pltpu.make_async_remote_copy(
-                src_ref=bo.at[s], dst_ref=dybuf.at[to], send_sem=b_send.at[s], recv_sem=b_recv.at[to],
-                device_id={'stage': prv}, device_id_type=MESH).start()
+            halves(m, lambda here, there: pltpu.make_async_copy(
+                bo.at[s], here.at[lax.rem(m, H)], pair_send.at[s]).start())
 
     table = [_words(row) for row in ORDER]
 
@@ -266,12 +268,12 @@
 
         @pl.when(kind == 2)
         def _():
+            ready_b(j)
             ready_f(i)
-            ready_b(j)
+            compute_b(j)
             compute_f(i)
-            compute_b(j)
+            done_b(j)
             done_f(i)
-            done_b(j)
 
         return i + jnp.where(kind == 1, 0, 1), j + jnp.where(kind == 0, 0, 1), bits // 4
 
@@ -286,14 +288,14 @@
         wait_b_send(jnp.int32(k))
         wait_uz(k % 2)
 
-    @pl.when(p == S - 2)
+    @pl.when(p == 1)
     def _():
         def take(m, c):
-            pltpu.make_async_copy(fo.at[0], hbuf.at[n + m], f_recv.at[n + m]).wait()
+            pltpu.make_async_copy(bo.at[0], dybuf.at[n + m], b_recv.at[n + m]).wait()
             return c
 
         lax.fori_loop(0, M, take, 0)
-        copies = [pltpu.make_async_copy(hbuf.at[pl.ds(n + k * H, H)], ref, pair_send.at[k]) for k, ref in enumerate((mine, other))]
+        copies = [pltpu.make_async_copy(dybuf.at[pl.ds(n + k * H, H)], ref, pair_send.at[k]) for k, ref in enumerate((other, mine))]
         for c in copies:
             c.start()
         for c in copies:
@@ -306,14 +308,19 @@
 
     lax.fori_loop(0, n, drain, 0)
 
-    @pl.when(p == 1)
+    @pl.when(p == S - 2)
     def _():
         lax.fori_loop(
             0, M, lambda m, c: (pltpu.make_async_copy(fo.at[0], mine.at[0], pair_recv.at[m]).wait(), c)[1], 0)
 
 
-def _grads(work, block, pieces, h, dz, u, dy, *rest):
-    d1, d2, narrow, wide, o1, o2, n_sem, w_sem, o_sem, p_sem = rest[-10:]
+def _grads(work, block, pieces, S, spread, h, dz, u, dy, *rest):
+    if spread:
+        parts = rest[2:5]
+        d1, d2, y, dx, narrow, wide, o1, o2, n_sem, w_sem, o_sem, p_sem, stage, s_sem = rest[-14:]
+        loads = [pltpu.make_async_copy(ref, stage.at[k], s_sem.at[k]) for k, ref in enumerate(parts)]
+    else:
+        d1, d2, narrow, wide, o1, o2, n_sem, w_sem, o_sem, p_sem = rest[-10:]
     T = wide.shape[1]
     begin = [sum(w[3] for w in work[:q]) for q in range(len(work) + 1)]
     total = begin[-1]
@@ -367,6 +374,9 @@
     wide_copy(jnp.int32(1), start)
     if len(work) > 1:
         narrow_copy(1, start)
+    if spread:
+        for c in loads:
+            c.start()
 
     piece(0, wait)
     o1[0] = lax.dot_general(narrow[0, :rows], wide[0, :rows], tn, preferred_element_type=F32)
@@ -379,6 +389,10 @@
 
     lax.fori_loop(1, pieces, add, jnp.int32(0))
     out_copy(jnp.int32(0), start)
+    if spread:
+        for c in loads:
+            c.wait()
+        _spread(S, [stage.at[k] for k in range(len(parts))], y, dx, s_sem)
 
     def step(s, carry):
         kind, _, _, slot = at(s)
@@ -413,26 +427,37 @@
     lax.fori_loop(1, total, step, jnp.int32(0))
     for s in (total - 2, total - 1):
         out_copy(jnp.int32(s), wait)
-
-
-def _grad(name, work, block, h, dz, u, dy, into=None):
+    if spread:
+        for k in range(len(parts)):
+            pltpu.make_async_copy(stage.at[k], y.at[pl.ds(0, stage.shape[1])], s_sem.at[k]).wait()
+
+
+def _grad(name, work, block, S, h, dz, u, dy, into=None, parts=None):
     V, T, D = h.shape
     F = dz.shape[-1]
     dma = pltpu.SemaphoreType.DMA
     pieces = 4
-    args = [h, dz, u, dy] + list(into or ())
+    hbm = pl.BlockSpec(memory_space=pltpu.HBM)
+    kinds = [w[0] for w in work]
+    args = [h, dz, u, dy] + list(into or ()) + list(parts or ())
+    outs = [jax.ShapeDtypeStruct((V, D, F), F32), jax.ShapeDtypeStruct((V, F, D), F32)]
+    scratch = [
+        pltpu.VMEM((2 if len(work) > 1 else 1, T, D), BF),
+        pltpu.VMEM((2, T, block), BF),
+        pltpu.VMEM((2, D, block), F32),
+        pltpu.VMEM((2, block, D) if 1 in kinds else (8, 128), F32),
+        dma((2,)), dma((2,)), dma((2,)), dma((2 * pieces,)),
+    ]
+    if parts:
+        H, B, _ = parts[0].shape
+        outs += [jax.ShapeDtypeStruct((2 * H, B, D), BF)] * 2
+        scratch += [pltpu.VMEM((len(parts), H, B, D), BF), dma((len(parts),))]
     return pl.pallas_call(
-        functools.partial(_grads, work, block, pieces),
-        out_shape=[jax.ShapeDtypeStruct((V, D, F), F32), jax.ShapeDtypeStruct((V, F, D), F32)],
-        in_specs=[pl.BlockSpec(memory_space=pl.ANY)] * len(args),
-        out_specs=[pl.BlockSpec(memory_space=pl.ANY)] * 2,
-        scratch_shapes=[
-            pltpu.VMEM((2, T, D), BF),
-            pltpu.VMEM((2, T, block), BF),
-            pltpu.VMEM((2, D, block), F32),
-            pltpu.VMEM((2, block, D), F32),
-            dma((2,)), dma((2,)), dma((2,)), dma((2 * pieces,)),
-        ],
+        functools.partial(_grads, work, block, pieces, S, bool(parts)),
+        out_shape=outs,
+        in_specs=[hbm] * len(args),
+        out_specs=[hbm] * len(outs),
+        scratch_shapes=scratch,
         input_output_aliases={4: 0, 5: 1} if into else {},
         compiler_params=pltpu.CompilerParams(vmem_limit_bytes=54 * 2 ** 20),
         cost_estimate=pl.CostEstimate(
@@ -441,29 +466,28 @@
     )(*args)
 
 
-def _assemble(S, M, mine, other, far, back, y, dx, sem):
+def _spread(S, parts, y, dx, sem, begin=0):
     p = lax.axis_index('stage')
     parity = lax.rem(p, 2)
     left = p < S // 2
-    H = M // 2
-
-    def put(src, k, dst, upper):
-        pltpu.make_async_copy(src, dst.at[pl.ds(upper * H, H)], sem.at[k]).start()
-
-    for k, src in enumerate((mine, other, far, back)):
-        upper = parity if k % 2 == 0 else 1 - parity
-        to_dx = left if k < 2 else jnp.logical_not(left)
+    for k, src in enumerate(parts):
+        H = src.shape[0]
+        upper = parity if (begin + k) % 2 == 0 else 1 - parity
+        to_dx = left if begin + k < 2 else jnp.logical_not(left)
+        rows = pl.ds(upper * H, H)
 
         @pl.when(to_dx)
         def _():
-            put(src, k, dx, upper)
+            pltpu.make_async_copy(src, dx.at[rows], sem.at[k]).start()
 
         @pl.when(jnp.logical_not(to_dx))
         def _():
-            put(src, k, y, upper)
-
-    for k in range(4):
-        pltpu.make_async_copy(mine, y.at[pl.ds(0, H)], sem.at[k]).wait()
+            pltpu.make_async_copy(src, y.at[rows], sem.at[k]).start()
+
+
+def _finish(S, back, y_in, dx_in, y, dx, sem):
+    _spread(S, [back], y, dx, sem, 3)
+    pltpu.make_async_copy(back, y.at[pl.ds(0, back.shape[0])], sem.at[0]).wait()
 
 
 def solution(mesh):
@@ -493,14 +517,14 @@
             scratch_shapes=[
                 pltpu.VMEM((V, D, F), BF),
                 pltpu.VMEM((V, F, D), BF),
+                pltpu.VMEM((n, B, D), BF),
                 pltpu.VMEM((n + M, B, D), BF),
-                pltpu.VMEM((n, B, D), BF),
                 pltpu.VMEM((B, F), BF),
                 pltpu.VMEM((2, B, F), BF),
                 pltpu.VMEM((2, B, F), BF),
                 pltpu.VMEM((2, B, D), BF),
                 pltpu.VMEM((2, B, D), BF),
-                dma((n + M,)), dma((n,)), dma((2,)), dma((2,)),
+                dma((n,)), dma((n + M,)), dma((2,)), dma((2,)),
                 dma((n,)), dma((n,)), dma((2,)), dma((2,)), dma((2 * V,)), dma((2,)), dma((M,)),
             ],
             compiler_params=pltpu.CompilerParams(
@@ -519,21 +543,24 @@
         block = 1024 if F % 1024 == 0 else F // 3 if F % 384 == 0 else F // 2
         nb = F // block
         work = [(0, 0, 0, nb)] + [(1, v, 0, nb) for v in range(V)] + [(0, v, 0, nb) for v in range(1, V - 1)]
-        d1, d2 = _grad('grads', work + [(0, V - 1, 0, nb - 2)] * (nb > 2), block, h, dz, u, dy)
+        d1, d2 = _grad('grads', work + [(0, V - 1, 0, nb - 2)] * (nb > 2), block, S, h, dz, u, dy)
         far, d1, d2 = lax.optimization_barrier((far, d1, d2))
         back = lax.ppermute(far, 'stage', [(q, q + 1 - 2 * (q % 2)) for q in range(S)])
-        d1, d2 = _grad('grads_last', [(0, V - 1, nb - 2, 2)], block, h, dz, u, dy, (d1, d2))
-        back, d1, d2 = lax.optimization_barrier((back, d1, d2))
+        d1, d2, y, dx = _grad(
+            'grads_last', [(0, V - 1, nb - 2, 2)], block, S, h, dz, u, dy, (d1, d2), (mine, other, far))
+        back, d1, d2, y, dx = lax.optimization_barrier((back, d1, d2, y, dx))
         full = jax.ShapeDtypeStruct((M, B, D), BF)
+        hbm = pl.BlockSpec(memory_space=pltpu.HBM)
         y, dx = pl.pallas_call(
-            functools.partial(_assemble, S, M),
+            functools.partial(_finish, S),
             out_shape=[full, full],
-            in_specs=[pl.BlockSpec(memory_space=pltpu.VMEM)] * 4,
-            out_specs=[anys] * 2,
-            scratch_shapes=[dma((4,))],
+            in_specs=[pl.BlockSpec(memory_space=pltpu.VMEM), hbm, hbm],
+            out_specs=[hbm, hbm],
+            scratch_shapes=[dma((1,))],
+            input_output_aliases={1: 0, 2: 1},
             compiler_params=pltpu.CompilerParams(vmem_limit_bytes=16 * 2 ** 20),
-            name='assemble',
-        )(mine, other, far, back)
+            name='last_quarter',
+        )(back, y, dx)
         return y, dx, d1[:, None], d2[:, None]
 
     act = P('data', None, None)

time: 394 us -> 403 us (1.023)
  Pallas kernels: 392 us -> 400 us
    pallas_call x1, Pallas kernels: 294 us -> 307 us  [body(): pl.pallas_call(functools.partial(_pipeline, S, V, M, G), out_shape=[jax.S...]
    pallas_call x3, Pallas kernels: 97.6 us -> 93.3 us  [the longest x2 91.6 us: _grad(): pl.pallas_call(functools.partial(_grads, work, block, pieces, S, bool(par...]
where the time goes in v5:
time: 403 us; the launch traced here: 402 us
  Pallas kernels  400 us (99%)
    pallas_call x1, Pallas kernels, body(): pl.pallas_call(functools.partial(_pipeline, S, V, M, G), out_shape=[jax.S...  307 us
    pallas_call x2, Pallas kernels, _grad(): pl.pallas_call(functools.partial(_grads, work, block, pieces, S, bool(par...  91.6 us
  transfers between devices with their start and end apart: 2, of which 0 were waited for; matrix products, arithmetic and copies ran while one was open for 0% of the time, Pallas kernels for 23%

profile of v5, /device:TPU:9, one launch (start us, length us, event | category | flops | bytes accessed | tf_op | source)
XLA Modules:
  0.0 402.4 jit_solution(1675833385692007381)
XLA Ops:
  0.6 306.5 %pipeline.1 = (bf16[32,256,3072]{2,1,0:T(8,128)(2,1)}, bf16[32,256,3072]{2,1,0:T(8,128)(2,1)}, bf16[32,256,768]{2,1,0:T(8,128)(2,1)}, bf16[32,256,768]{2,1,0:T(8...) custom-call(bf16[16,256,768]{2,1,0:T(8,128)(2,1)} %x.1, bf16[16,256,768]{2,1,0:T(8,128)(2,1)} %g.1, ...), custom_call_target="tpu_custom_call" | custom-call | flops 193273528320 | bytes 100663296 | tf_op jit(solution)/shard_map/pipeline/pallas_call | solution.py:506
  307.2 0.0 collective-permute-start
  307.2 72.7 %grads.1 = (f32[2,768,3072]{2,1,0:T(8,128)}, f32[2,3072,768]{2,1,0:T(8,128)}) custom-call(bf16[2,4096,768]{2,1,0:T(8,128)(2,1)} %bitcast.18, bf16[2,4096,3072]{2,1,0:T(8,128)(2,1)} %bitcast.14, bf16[2,4096,3072]{2,1,0:T(8,128)(2,1)} %bitcast.12, bf16[2,4096,768]{2,1,0:T(8,128)(2,1)} %bitcast.20), custom_call_target="tpu_custom_call" | custom-call | flops 64424509440 | bytes 115343360 | tf_op jit(solution)/shard_map/grads/pallas_call | solution.py:455
  379.9 0.0 collective-permute-done.rest_4_
  380.0 0.0 copy-start
  380.0 0.0 collective-permute-start.1
  380.0 1.6 copy-done
  381.6 18.9 %grads_last.1 = (f32[2,768,3072]{2,1,0:T(8,128)}, f32[2,3072,768]{2,1,0:T(8,128)}, bf16[16,256,768]{2,1,0:T(8,128)(2,1)}, bf16[16,256,768]{2,1,0:T(8,128)(2,1)}) custom-call(bf16[2,4096,768]{2,1,0:T(8,128)(2,1)} %bitcast.19, bf16[2,4096,3072]{2,1,0:T(8,128)(2,1)} %bitcast.15, ...), custom_call_target="tpu_custom_call", output_to_operand_aliasing={{0}: (4, {}), {1}: (5, {})} | custom-call | flops 12884901888 | bytes 23068672 | tf_op jit(solution)/shard_map/grads_last/pallas_call | solution.py:455
  400.5 0.0 collective-permute-done.1.back
  400.5 1.7 last_quarter.1
Async XLA Ops:
  307.2 72.8 %collective-permute-start = (bf16[8,256,768]{2,1,0:T(8,128)(2,1)}, bf16[8,256,768]{2,1,0:T(8,128)(2,1)S(1)}, u32[]{:S(2)}, u32[]{:S(2)}) collective-permute-start(bf16[8,256,768]{2,1,0:T(8,128)(2,1)} %get-tuple-element.26.rest_2_), channel_id=1, source_target_pairs={{0,2},{1,3},{2,0},{3,1},{4,6},{5,7},{6,4},{7,5},{8,10},{9,11},{10,... | collective-permute-start | bytes 9437192 | tf_op jit(solution)/shard_map/ppermute | solution.py:542
  380.0 1.7 copy-start
  380.0 20.5 %collective-permute-start.1 = (bf16[8,256,768]{2,1,0:T(8,128)(2,1)S(1)}, bf16[8,256,768]{2,1,0:T(8,128)(2,1)S(1)}, u32[]{:S(2)}, u32[]{:S(2)}) collective-permute-start(bf16[8,256,768]{2,1,0:T(8,128)(2,1)S(1)} %collective-permute-done.rest_4_), channel_id=1, source_target_pairs={{0,1},{1,0},{2,3},{3,2},{4,5},{5,4},{6,7},{7,6},{8,9},{9,8},{10,11... | collective-permute-start | bytes 9437192 | tf_op jit(solution)/shard_map/ppermute | solution.py:548

commit v6 on v5

--- a/solution.py
+++ b/solution.py
@@ -13,12 +13,12 @@
 NT = (((1,), (1,)), ((), ()))
 GROUP = 8
 ORDER = (
-    'FFFFFFFFFFFFFFFFFFFFFBFMBBFBFBFBFBBFBFFBFBFBBBBBBBBBBBBBBBBBBBB',
-    'FFFFFFFFFFFFFFFFFFBFFMBBBFBFBFBFBMFBFMFBFMBBBBBBBBBBBBBBBBBB',
-    'FFFFFFFFFFFBFMFMMMMMMMMMMMBMMMMMMMBBBBBBBBBBB',
-    'FFFFFFFFBFBMBBBMBFFBFBMBMFMMFFMMMMMBMMBBBBBBBBBFFFF',
+    'FFFFFFFFFFFFFFFFFFFFBFBFBFBBFBBFFBBFFFBBFFBFBBBBBBBBBBBBBBBBBBBB',
+    'FFFFFFFFFFFFFFFFFBFBBFFFFBBBFFBBBFBFFFBFBFBFBFBBBBBBBBBBBBBBBBBB',
+    'FFFFFFFFFFFBBFFBFBFFBBBBBFFFBFFFBBFFBBFBFBFBFFFBBFBBFBBBBBBBBBBB',
+    'FFFFFFFFBBFFBBBFBBBBFBBFFFBFBFBFFBFFBFBBFBFBFFBBFBBBBBBBBBBFFFFF',
 )
-WORD = 15
+WORD = 16
 
 
 def _gelu(z):
@@ -39,7 +39,7 @@
 
 
 def _words(row):
-    return [sum('FBM'.index(c) * 4 ** b for b, c in enumerate(row[k:k + WORD])) for k in range(0, len(row), WORD)]
+    return [sum('FB'.index(c) * 2 ** b for b, c in enumerate(row[k:k + WORD])) for k in range(0, len(row), WORD)]
 
 
 def _pipeline(S, V, M, G, x, g, w1_hbm, w2_hbm, u_out, dz_out, h_out, dy_out, mine, other,
@@ -252,7 +252,7 @@
     def step(t, carry):
         i, j, bits = carry
         bits = jnp.where(lax.rem(t, WORD) == 0, word(t // WORD), bits)
-        kind = lax.rem(bits, 4)
+        kind = lax.rem(bits, 2)
 
         @pl.when(kind == 0)
         def _():
@@ -266,22 +266,10 @@
             compute_b(j)
             done_b(j)
 
-        @pl.when(kind == 2)
-        def _():
-            ready_b(j)
-            ready_f(i)
-            compute_b(j)
-            compute_f(i)
-            done_b(j)
-            done_f(i)
-
-        return i + jnp.where(kind == 1, 0, 1), j + jnp.where(kind == 0, 0, 1), bits // 4
+        return i + 1 - kind, j + kind, bits // 2
 
     zero = jnp.int32(0)
-    count = jnp.int32(0)
-    for q in range(S):
-        count = jnp.where(p == q, len(ORDER[q]), count)
-    lax.fori_loop(0, count, step, (zero, zero, zero))
+    lax.fori_loop(0, 2 * n, step, (zero, zero, zero))
 
     for k in (n - 2, n - 1):
         wait_f_send(jnp.int32(k))

time: 403 us -> 393 us (0.975)
  Pallas kernels: 400 us -> 390 us
    pallas_call x1, Pallas kernels: 307 us -> 296 us  [body(): pl.pallas_call(functools.partial(_pipeline, S, V, M, G), out_shape=[jax.S...]
where the time goes in v6:
time: 393 us; the launch traced here: 392 us
  Pallas kernels  390 us (99%)
    pallas_call x1, Pallas kernels, body(): pl.pallas_call(functools.partial(_pipeline, S, V, M, G), out_shape=[jax.S...  296 us
    pallas_call x2, Pallas kernels, _grad(): pl.pallas_call(functools.partial(_grads, work, block, pieces, S, bool(par...  91.8 us
  transfers between devices with their start and end apart: 2, of which 0 were waited for; matrix products, arithmetic and copies ran while one was open for 0% of the time, Pallas kernels for 23%

profile of v6, /device:TPU:9, one launch (start us, length us, event | category | flops | bytes accessed | tf_op | source)
XLA Modules:
  0.0 392.2 jit_solution(7954790357607682232)
XLA Ops:
  0.6 296.2 %pipeline.1 = (bf16[32,256,3072]{2,1,0:T(8,128)(2,1)}, bf16[32,256,3072]{2,1,0:T(8,128)(2,1)}, bf16[32,256,768]{2,1,0:T(8,128)(2,1)}, bf16[32,256,768]{2,1,0:T(8...) custom-call(bf16[16,256,768]{2,1,0:T(8,128)(2,1)} %x.1, bf16[16,256,768]{2,1,0:T(8,128)(2,1)} %g.1, ...), custom_call_target="tpu_custom_call" | custom-call | flops 193273528320 | bytes 100663296 | tf_op jit(solution)/shard_map/pipeline/pallas_call | solution.py:494
  296.8 0.0 collective-permute-start
  296.9 72.9 %grads.1 = (f32[2,768,3072]{2,1,0:T(8,128)}, f32[2,3072,768]{2,1,0:T(8,128)}) custom-call(bf16[2,4096,768]{2,1,0:T(8,128)(2,1)} %bitcast.18, bf16[2,4096,3072]{2,1,0:T(8,128)(2,1)} %bitcast.14, bf16[2,4096,3072]{2,1,0:T(8,128)(2,1)} %bitcast.12, bf16[2,4096,768]{2,1,0:T(8,128)(2,1)} %bitcast.20), custom_call_target="tpu_custom_call" | custom-call | flops 64424509440 | bytes 115343360 | tf_op jit(solution)/shard_map/grads/pallas_call | solution.py:443
  369.8 0.0 collective-permute-done.rest_4_
  369.8 0.0 copy-start
  369.8 0.0 collective-permute-start.1
  369.8 1.6 copy-done
  371.4 18.9 %grads_last.1 = (f32[2,768,3072]{2,1,0:T(8,128)}, f32[2,3072,768]{2,1,0:T(8,128)}, bf16[16,256,768]{2,1,0:T(8,128)(2,1)}, bf16[16,256,768]{2,1,0:T(8,128)(2,1)}) custom-call(bf16[2,4096,768]{2,1,0:T(8,128)(2,1)} %bitcast.19, bf16[2,4096,3072]{2,1,0:T(8,128)(2,1)} %bitcast.15, ...), custom_call_target="tpu_custom_call", output_to_operand_aliasing={{0}: (4, {}), {1}: (5, {})} | custom-call | flops 12884901888 | bytes 23068672 | tf_op jit(solution)/shard_map/grads_last/pallas_call | solution.py:443
  390.3 0.0 collective-permute-done.1.back
  390.3 1.7 last_quarter.1
Async XLA Ops:
  296.8 73.0 %collective-permute-start = (bf16[8,256,768]{2,1,0:T(8,128)(2,1)}, bf16[8,256,768]{2,1,0:T(8,128)(2,1)S(1)}, u32[]{:S(2)}, u32[]{:S(2)}) collective-permute-start(bf16[8,256,768]{2,1,0:T(8,128)(2,1)} %get-tuple-element.26.rest_2_), channel_id=1, source_target_pairs={{0,2},{1,3},{2,0},{3,1},{4,6},{5,7},{6,4},{7,5},{8,10},{9,11},{10,... | collective-permute-start | bytes 9437192 | tf_op jit(solution)/shard_map/ppermute | solution.py:530
  369.8 1.7 copy-start
  369.8 20.5 %collective-permute-start.1 = (bf16[8,256,768]{2,1,0:T(8,128)(2,1)S(1)}, bf16[8,256,768]{2,1,0:T(8,128)(2,1)S(1)}, u32[]{:S(2)}, u32[]{:S(2)}) collective-permute-start(bf16[8,256,768]{2,1,0:T(8,128)(2,1)S(1)} %collective-permute-done.rest_4_), channel_id=1, source_target_pairs={{0,1},{1,0},{2,3},{3,2},{4,5},{5,4},{6,7},{7,6},{8,9},{9,8},{10,11... | collective-permute-start | bytes 9437192 | tf_op jit(solution)/shard_map/ppermute | solution.py:536

commit v7 on v6

--- a/solution.py
+++ b/solution.py
@@ -13,10 +13,10 @@
 NT = (((1,), (1,)), ((), ()))
 GROUP = 8
 ORDER = (
-    'FFFFFFFFFFFFFFFFFFFFBFBFBFBBFBBFFBBFFFBBFFBFBBBBBBBBBBBBBBBBBBBB',
-    'FFFFFFFFFFFFFFFFFBFBBFFFFBBBFFBBBFBFFFBFBFBFBFBBBBBBBBBBBBBBBBBB',
-    'FFFFFFFFFFFBBFFBFBFFBBBBBFFFBFFFBBFFBBFBFBFBFFFBBFBBFBBBBBBBBBBB',
-    'FFFFFFFFBBFFBBBFBBBBFBBFFFBFBFBFFBFFBFBBFBFBFFBBFBBBBBBBBBBFFFFF',
+    'FFFFFFFFFFFFFFFFFFFFFFFBFBBBBFBFBFBFBFBFBFBFBBBBBBBBBBBBBBBBBBBB',
+    'FFFFFFFFFFFFFFFFFFFBFBFBFBFBFBBFBFBFBFBFBFBFBFBBBBBBBBBBBBBBBBBB',
+    'FFFFFFFFFFFBFFBFBFBFBFBFBFBFBFBFBFBFBFBFBFBFBFBFBFBFBBBBBBBBBBBB',
+    'FFFFFFFFBBBFBBFBFBFBBFFFBFBFBFBFBFBFBBFBFBFBFBFBFBFBBBBBFBBBBFFF',
 )
 WORD = 16
 
@@ -229,16 +229,27 @@
         slot = v * M + m
         s = lax.rem(j, 2)
         final = first & (v == 0)
-        to = jnp.where(final, n + m, slot - jnp.where(first, M, 0))
-        pltpu.make_async_remote_copy(
-            src_ref=bo.at[s], dst_ref=dybuf.at[to], send_sem=b_send.at[s], recv_sem=b_recv.at[to],
-            device_id={'stage': jnp.where(final, partner, prv)}, device_id_type=MESH).start()
+
+        @pl.when(final)
+        def _():
+            k = lax.rem(m, H)
+
+            def put(here, there):
+                pltpu.make_async_copy(bo.at[s], here.at[k], b_send.at[s]).start()
+                pltpu.make_async_remote_copy(
+                    src_ref=bo.at[s], dst_ref=there.at[k], send_sem=pair_send.at[s], recv_sem=pair_recv.at[m],
+                    device_id={'stage': partner}, device_id_type=MESH).start()
+
+            halves(m, put)
+
+        @pl.when(jnp.logical_not(final))
+        def _():
+            to = slot - jnp.where(first, M, 0)
+            pltpu.make_async_remote_copy(
+                src_ref=bo.at[s], dst_ref=dybuf.at[to], send_sem=b_send.at[s], recv_sem=b_recv.at[to],
+                device_id={'stage': prv}, device_id_type=MESH).start()
+
         pltpu.make_async_copy(dzb.at[s], dz_out.at[slot], dz_sem.at[s]).start()
-
-        @pl.when(final)
-        def _():
-            halves(m, lambda here, there: pltpu.make_async_copy(
-                bo.at[s], here.at[lax.rem(m, H)], pair_send.at[s]).start())
 
     table = [_words(row) for row in ORDER]
 
@@ -276,19 +287,6 @@
         wait_b_send(jnp.int32(k))
         wait_uz(k % 2)
 
-    @pl.when(p == 1)
-    def _():
-        def take(m, c):
-            pltpu.make_async_copy(bo.at[0], dybuf.at[n + m], b_recv.at[n + m]).wait()
-            return c
-
-        lax.fori_loop(0, M, take, 0)
-        copies = [pltpu.make_async_copy(dybuf.at[pl.ds(n + k * H, H)], ref, pair_send.at[k]) for k, ref in enumerate((other, mine))]
-        for c in copies:
-            c.start()
-        for c in copies:
-            c.wait()
-
     def drain(slot, carry):
         pltpu.make_async_copy(hbuf.at[slot], h_out.at[slot], h_sem.at[slot]).wait()
         pltpu.make_async_copy(dybuf.at[slot], dy_out.at[slot], dy_sem.at[slot]).wait()
@@ -296,7 +294,7 @@
 
     lax.fori_loop(0, n, drain, 0)
 
-    @pl.when(p == S - 2)
+    @pl.when(jnp.logical_not(first | last))
     def _():
         lax.fori_loop(
             0, M, lambda m, c: (pltpu.make_async_copy(fo.at[0], mine.at[0], pair_recv.at[m]).wait(), c)[1], 0)
@@ -506,13 +504,13 @@
                 pltpu.VMEM((V, D, F), BF),
                 pltpu.VMEM((V, F, D), BF),
                 pltpu.VMEM((n, B, D), BF),
-                pltpu.VMEM((n + M, B, D), BF),
+                pltpu.VMEM((n, B, D), BF),
                 pltpu.VMEM((B, F), BF),
                 pltpu.VMEM((2, B, F), BF),
                 pltpu.VMEM((2, B, F), BF),
                 pltpu.VMEM((2, B, D), BF),
                 pltpu.VMEM((2, B, D), BF),
-                dma((n,)), dma((n + M,)), dma((2,)), dma((2,)),
+                dma((n,)), dma((n,)), dma((2,)), dma((2,)),
                 dma((n,)), dma((n,)), dma((2,)), dma((2,)), dma((2 * V,)), dma((2,)), dma((M,)),
             ],
             compiler_params=pltpu.CompilerParams(

time: 393 us -> 389 us (0.990)
  Pallas kernels: 390 us -> 386 us
  transfers between devices with their start and end apart: 2 -> 2, of which waited for: 0 -> 0; matrix products, arithmetic and copies ran while one was open for 0% -> 0% of each run, Pallas kernels for 23% -> 24%
where the time goes in v7:
time: 389 us; the launch traced here: 388 us
  Pallas kernels  386 us (99%)
    pallas_call x1, Pallas kernels, body(): pl.pallas_call(functools.partial(_pipeline, S, V, M, G), out_shape=[jax.S...  292 us
    pallas_call x2, Pallas kernels, _grad(): pl.pallas_call(functools.partial(_grads, work, block, pieces, S, bool(par...  91.7 us
  transfers between devices with their start and end apart: 2, of which 0 were waited for; matrix products, arithmetic and copies ran while one was open for 0% of the time, Pallas kernels for 24%

profile of v7, /device:TPU:9, one launch (start us, length us, event | category | flops | bytes accessed | tf_op | source)
XLA Modules:
  0.0 388.3 jit_solution(7022125062723310615)
XLA Ops:
  0.6 292.3 %pipeline.1 = (bf16[32,256,3072]{2,1,0:T(8,128)(2,1)}, bf16[32,256,3072]{2,1,0:T(8,128)(2,1)}, bf16[32,256,768]{2,1,0:T(8,128)(2,1)}, bf16[32,256,768]{2,1,0:T(8...) custom-call(bf16[16,256,768]{2,1,0:T(8,128)(2,1)} %x.1, bf16[16,256,768]{2,1,0:T(8,128)(2,1)} %g.1, ...), custom_call_target="tpu_custom_call" | custom-call | flops 193273528320 | bytes 100663296 | tf_op jit(solution)/shard_map/pipeline/pallas_call | solution.py:492
  293.0 0.0 collective-permute-start
  293.0 72.9 %grads.1 = (f32[2,768,3072]{2,1,0:T(8,128)}, f32[2,3072,768]{2,1,0:T(8,128)}) custom-call(bf16[2,4096,768]{2,1,0:T(8,128)(2,1)} %bitcast.18, bf16[2,4096,3072]{2,1,0:T(8,128)(2,1)} %bitcast.14, bf16[2,4096,3072]{2,1,0:T(8,128)(2,1)} %bitcast.12, bf16[2,4096,768]{2,1,0:T(8,128)(2,1)} %bitcast.20), custom_call_target="tpu_custom_call" | custom-call | flops 64424509440 | bytes 115343360 | tf_op jit(solution)/shard_map/grads/pallas_call | solution.py:441
  365.9 0.0 collective-permute-done.rest_4_
  365.9 0.0 copy-start
  365.9 0.5 collective-permute-start.1
  366.4 1.2 copy-done
  367.6 18.9 %grads_last.1 = (f32[2,768,3072]{2,1,0:T(8,128)}, f32[2,3072,768]{2,1,0:T(8,128)}, bf16[16,256,768]{2,1,0:T(8,128)(2,1)}, bf16[16,256,768]{2,1,0:T(8,128)(2,1)}) custom-call(bf16[2,4096,768]{2,1,0:T(8,128)(2,1)} %bitcast.19, bf16[2,4096,3072]{2,1,0:T(8,128)(2,1)} %bitcast.15, ...), custom_call_target="tpu_custom_call", output_to_operand_aliasing={{0}: (4, {}), {1}: (5, {})} | custom-call | flops 12884901888 | bytes 23068672 | tf_op jit(solution)/shard_map/grads_last/pallas_call | solution.py:441
  386.5 0.0 collective-permute-done.1.back
  386.5 1.7 last_quarter.1
Async XLA Ops:
  293.0 72.9 %collective-permute-start = (bf16[8,256,768]{2,1,0:T(8,128)(2,1)}, bf16[8,256,768]{2,1,0:T(8,128)(2,1)S(1)}, u32[]{:S(2)}, u32[]{:S(2)}) collective-permute-start(bf16[8,256,768]{2,1,0:T(8,128)(2,1)} %get-tuple-element.26.rest_2_), channel_id=1, source_target_pairs={{0,2},{1,3},{2,0},{3,1},{4,6},{5,7},{6,4},{7,5},{8,10},{9,11},{10,... | collective-permute-start | bytes 9437192 | tf_op jit(solution)/shard_map/ppermute | solution.py:528
  365.9 1.7 copy-start
  365.9 20.5 %collective-permute-start.1 = (bf16[8,256,768]{2,1,0:T(8,128)(2,1)S(1)}, bf16[8,256,768]{2,1,0:T(8,128)(2,1)S(1)}, u32[]{:S(2)}, u32[]{:S(2)}) collective-permute-start(bf16[8,256,768]{2,1,0:T(8,128)(2,1)S(1)} %collective-permute-done.rest_4_), channel_id=1, source_target_pairs={{0,1},{1,0},{2,3},{3,2},{4,5},{5,4},{6,7},{7,6},{8,9},{9,8},{10,11... | collective-permute-start | bytes 9437192 | tf_op jit(solution)/shard_map/ppermute | solution.py:534
